TPU v7x, 512 devices: a whole 4x8x8 slice. The times are simulated.
512 devices in a mesh: va: 16 (over z_hi, y), vb: 8 (over z_lo, core), occ: 4 (over x).
Axes of the slice: x: 4, y: 8, z: 8 (z_hi: 2, z_lo: 4; z = z_hi * 4 + z_lo), core: 2. Of those that a mesh axis runs over, the one named last changes fastest.
Arguments:
- amplitudes: bfloat16 [6, 1536, 1536], P(None, 'va', 'occ'), may hold values from -6 to 6
- bra_factor: bfloat16 [16, 1536, 1536], P('vb', 'va'), may hold values from -0.078125 to 0.078125
- ket_factor: bfloat16 [16, 1536, 1536], P('va', ('vb', 'occ')), may hold values from -0.15625 to 0.15625
- pair_list: int32 [8, 4], replicated, may hold values from 0 to 5, as said below
Outputs:
- ladder: float32 [6, 1536, 1536], P(None, 'va', ('vb', 'occ'))
Inputs may be any that keep to these rules, and one draw needn't show every extreme that they name: `pair_list`: each row names 4 different pairs, and every pair of 0 to 5 is named by some row.
All inputs are finite; a program needn't handle non-finite values.
Results may differ from a plain program's by a relative error of at most 0.0042.
Values may be sent and summed in bfloat16 or wider, within the bound.
No kernel may reach another device: no remote copies, remote signals or barrier semaphores. Data moves between devices by JAX's collectives and lax.ppermute only.
A program may use at most 64 MiB of HBM per device.

v0:
```python
import jax
import jax.numpy as jnp
from jax import lax
from jax.sharding import Mesh
from jax.sharding import PartitionSpec as P

VA = ("va_0", "va_1")


def from_everyone(array, axis):
    copies = jnp.broadcast_to(array, (lax.axis_size(axis), *array.shape))
    return lax.all_to_all(copies, axis, split_axis=0, concat_axis=0, tiled=True)


def laid_out(blocks, dim):
    blocks = jnp.moveaxis(blocks, 0, dim)
    lengths = blocks.shape
    return blocks.reshape(*lengths[:dim], lengths[dim] * lengths[dim + 1], *lengths[dim + 2 :])


def gather_directly(array, axis, dim):
    blocks = from_everyone(array, axis)
    return laid_out(blocks, dim)


def stacked_from(array, axes, turns):
    blocks = array
    for k in turns:
        blocks = lax.all_gather(blocks, axes[k])
    done = turns[::-1]
    back = [done.index(k) for k in range(len(axes))]
    blocks = blocks.transpose(*back, *range(len(axes), blocks.ndim))
    return blocks.reshape(-1, *array.shape)


def whole_of(array, axes, turns, dim):
    return laid_out(stacked_from(array, axes, turns), dim)


def from_behind(block, axis, distance):
    devices = range(lax.axis_size(axis))
    route = [((i - distance) % len(devices), i) for i in devices]
    return lax.ppermute(block, axis, route)


def cut_along(array, dim, devices):
    before, after = (array.shape[:dim], array.shape[dim + 1 :])
    return jnp.moveaxis(array.reshape(*before, devices, -1, *after), dim, 0)


def sent_and_summed(array, axis, dim):
    devices = lax.axis_size(axis)
    blocks = lax.all_to_all(cut_along(array, dim, devices), axis, 0, 0, tiled=True)
    return jnp.sum(blocks.astype(jnp.float32), axis=0)


def per_device(amplitudes, bra_factor, ket_factor, pair_list):
    tau_rows = gather_directly(amplitudes, "occ", 2)
    ket_rows = whole_of(ket_factor, VA, (0, 1), 0)
    group = bra_factor.shape[0]
    pairs = amplitudes.shape[0]
    cycle_size = lax.axis_size("vb")
    position = lax.axis_index("vb")

    def contribute(total, bra_block, which):
        picks = lax.dynamic_index_in_dim(pair_list, which, 0, keepdims=False)
        chosen = jnp.take(tau_rows, picks, axis=0)
        ket_group = lax.dynamic_slice_in_dim(ket_rows, which * group, group, 0)
        half = jnp.einsum(
            "qbd,kcd->qkcb", ket_group, chosen, preferred_element_type=jnp.float32
        ).astype(jnp.bfloat16)
        partial_terms = jnp.einsum(
            "qca,qkcb->kab", bra_block, half, preferred_element_type=jnp.float32
        )
        return total.at[picks].add(partial_terms)

    total = jnp.zeros((pairs, bra_factor.shape[2], ket_factor.shape[1]), jnp.float32)
    total = contribute(total, bra_factor, position % cycle_size)
    forward = bra_factor
    backward = bra_factor
    for step in range(1, cycle_size // 2 + 1):
        forward = from_behind(forward, "vb", 1)
        total = contribute(total, forward, (position - step) % cycle_size)
        if step < cycle_size - step:
            backward = from_behind(backward, "vb", -1)
            total = contribute(total, backward, (position + step) % cycle_size)
    return sent_and_summed(total.astype(jnp.bfloat16), VA, 1)


def solution(mesh):
    torus = Mesh(
        mesh.devices.reshape(2, 8, mesh.shape["vb"], mesh.shape["occ"]),
        ("va_0", "va_1", "vb", "occ"),
    )
    return jax.shard_map(
        per_device,
        mesh=torus,
        in_specs=(P(None, VA, "occ"), P("vb", VA, None), P(VA, ("vb", "occ"), None), P()),
        out_specs=P(None, VA, ("vb", "occ")),
        check_vma=False,
    )
```

profile of v0, /device:TPU:15, one launch (start us, length us, event | category | flops | bytes accessed | tf_op | source)
XLA Modules:
  0.0 190.2 jit_solution(15943147868413407421)
XLA Ops:
  6.5 4.6 %collective-permute-start = (bf16[2,96,1536]{2,1,0:T(8,128)(2,1)}, bf16[2,96,1536]{2,1,0:T(8,128)(2,1)S(1)}, u32[]{:S(2)}, u32[]{:S(2)}) collective-permute-start(bf16[2,96,1536]{2,1,0:T(8,128)(2,1)} %param.7), channel_id=1, source_target_pairs={{28,0},{0,4},{4,8},{8,12},{12,16},{16,20},{20,24},{24,28},{29,1},{... | collective-permute-start | bytes 1769480 | tf_op jit(solution)/shard_map/ppermute | solution.py:43
  11.1 1.9 %collective-permute-start.1 = (bf16[2,96,1536]{2,1,0:T(8,128)(2,1)}, bf16[2,96,1536]{2,1,0:T(8,128)(2,1)S(1)}, u32[]{:S(2)}, u32[]{:S(2)}) collective-permute-start(bf16[2,96,1536]{2,1,0:T(8,128)(2,1)} %param.7), channel_id=1, source_target_pairs={{4,0},{8,4},{12,8},{16,12},{20,16},{24,20},{28,24},{0,28},{5,1},{9... | collective-permute-start | bytes 1769480 | tf_op jit(solution)/shard_map/ppermute | solution.py:43
  13.0 2.4 %broadcast_in_dim.14 = bf16[4,6,96,384]{3,2,1,0:T(8,128)(2,1)} broadcast(bf16[6,96,384]{2,1,0:T(8,128)(2,1)} %param.6), dimensions={1,2,3} | broadcast | bytes 2211840 | tf_op jit(solution)/shard_map/broadcast_in_dim | solution.py:11
  15.4 4.3 %all-to-all-start = ((bf16[4,6,96,384]{3,2,1,0:T(8,128)(2,1)}), bf16[4,6,96,384]{3,2,1,0:T(8,128)(2,1)S(1)}, u32[]{:S(2)}, u32[]{:S(2)}) async-start(bf16[4,6,96,384]{3,2,1,0:T(8,128)(2,1)} %broadcast_in_dim.14), calls=%async_computation | async-start | bytes 3538944 | tf_op jit(solution)/shard_map/all_to_all | solution.py:12
  19.8 12.8 %all-gather = bf16[2,48,1536]{2,1,0:T(8,128)(2,1)} all-gather(bf16[1,48,1536]{2,1,0:T(8,128)(2,1)S(1)} %copy-done.3), channel_id=2, replica_groups=mesh['va_0'=2,'va_1'=8,'vb'=8,'occ'=4] {'va_0'}, dimensions={0}, use_global_device_ids=true | all-gather | bytes 442368 | tf_op jit(solution)/shard_map/all_gather | solution.py:29
  40.0 11.1 %collective-permute-start.2 = (bf16[2,96,1536]{2,1,0:T(8,128)(2,1)S(1)}, bf16[2,96,1536]{2,1,0:T(8,128)(2,1)}, u32[]{:S(2)}, u32[]{:S(2)}) collective-permute-start(bf16[2,96,1536]{2,1,0:T(8,128)(2,1)S(1)} %collective-permute-done), channel_id=1, source_target_pairs={{28,0},{0,4},{4,8},{8,12},{12,16},{16,20},{20,24},{24,28},{29,1},{... | collective-permute-start | bytes 1769480 | tf_op jit(solution)/shard_map/ppermute | solution.py:43
  52.9 1.9 %collective-permute-start.3 = (bf16[2,96,1536]{2,1,0:T(8,128)(2,1)S(1)}, bf16[2,96,1536]{2,1,0:T(8,128)(2,1)}, u32[]{:S(2)}, u32[]{:S(2)}) collective-permute-start(bf16[2,96,1536]{2,1,0:T(8,128)(2,1)S(1)} %collective-permute-done.1), channel_id=1, source_target_pairs={{4,0},{8,4},{12,8},{16,12},{20,16},{24,20},{28,24},{0,28},{5,1},{9... | collective-permute-start | bytes 1769480 | tf_op jit(solution)/shard_map/ppermute | solution.py:43
  54.9 6.9 %collective-permute-done.2 = bf16[2,96,1536]{2,1,0:T(8,128)(2,1)} collective-permute-done((bf16[2,96,1536]{2,1,0:T(8,128)(2,1)S(1)}, bf16[2,96,1536]{2,1,0:T(8,128)(2,1)}, u32[]{:S(2)}, u32[]{:S(2)}) %collective-permute-start.2) | collective-permute-done | bytes 589856 | tf_op jit(solution)/shard_map/ppermute | solution.py:43
  61.8 4.5 %collective-permute-start.4 = (bf16[2,96,1536]{2,1,0:T(8,128)(2,1)}, bf16[2,96,1536]{2,1,0:T(8,128)(2,1)}, u32[]{:S(2)}, u32[]{:S(2)}) collective-permute-start(bf16[2,96,1536]{2,1,0:T(8,128)(2,1)} %collective-permute-done.2), channel_id=1, source_target_pairs={{28,0},{0,4},{4,8},{8,12},{12,16},{16,20},{20,24},{24,28},{29,1},{... | collective-permute-start | bytes 1769480 | tf_op jit(solution)/shard_map/ppermute | solution.py:43
  68.6 2.3 %collective-permute-done.3 = bf16[2,96,1536]{2,1,0:T(8,128)(2,1)} collective-permute-done((bf16[2,96,1536]{2,1,0:T(8,128)(2,1)S(1)}, bf16[2,96,1536]{2,1,0:T(8,128)(2,1)}, u32[]{:S(2)}, u32[]{:S(2)}) %collective-permute-start.3) | collective-permute-done | bytes 589856 | tf_op jit(solution)/shard_map/ppermute | solution.py:43
  70.9 1.9 %collective-permute-start.5 = (bf16[2,96,1536]{2,1,0:T(8,128)(2,1)}, bf16[2,96,1536]{2,1,0:T(8,128)(2,1)}, u32[]{:S(2)}, u32[]{:S(2)}) collective-permute-start(bf16[2,96,1536]{2,1,0:T(8,128)(2,1)} %collective-permute-done.3), channel_id=1, source_target_pairs={{4,0},{8,4},{12,8},{16,12},{20,16},{24,20},{28,24},{0,28},{5,1},{9... | collective-permute-start | bytes 1769480 | tf_op jit(solution)/shard_map/ppermute | solution.py:43
  79.7 1.8 gather_fusion.4
  83.2 1.8 gather_fusion.6
  85.8 3.8 %collective-permute-start.6 = (bf16[2,96,1536]{2,1,0:T(8,128)(2,1)}, bf16[2,96,1536]{2,1,0:T(8,128)(2,1)}, u32[]{:S(2)}, u32[]{:S(2)}) collective-permute-start(bf16[2,96,1536]{2,1,0:T(8,128)(2,1)} %collective-permute-done.4), channel_id=1, source_target_pairs={{28,0},{0,4},{4,8},{8,12},{12,16},{16,20},{20,24},{24,28},{29,1},{... | collective-permute-start | bytes 1769480 | tf_op jit(solution)/shard_map/ppermute | solution.py:43
  89.6 1.8 copy.7
  91.5 4.2 %convolution_bitcast_fusion.7 = f32[4,1536,48]{1,2,0:T(8,128)} fusion(bf16[4,96,1536]{2,1,0:T(8,128)(2,1)} %gather_fusion, pred[4]{0:T(512)(128)(4,1)S(1)} %copy-done.8, bf16[2,96,1536]{2,1,0:T(8,128)(2,1)} %param.7, bf16[16,48,1536]{2,1,0:T(8,128)(2,1)S(1)} %bitcast.268, s32[]{:T(128)S(6)} %select_n.174), kind=kOutput, calls=%fused_computation.23 | convolution fusion | flops 227119104 | bytes 3244548 | tf_op jit(solution)/shard_map/qca,qkcb->kab/dot_general | solution.py:72
  95.8 3.4 %convolution_bitcast_fusion.6 = f32[4,1536,48]{1,2,0:T(8,128)} fusion(bf16[4,96,1536]{2,1,0:T(8,128)(2,1)} %gather_fusion.1, pred[4]{0:T(512)(128)(4,1)S(1)} %copy-done.9, bf16[2,96,1536]{2,1,0:T(8,128)(2,1)} %copy-done.2, bf16[16,48,1536]{2,1,0:T(8,128)(2,1)S(1)} %bitcast.269, s32[]{:T(128)S(6)} %select_n.178), kind=kOutput, calls=%fused_computation.22 | convolution fusion | flops 227119104 | bytes 3244548 | tf_op jit(solution)/shard_map/qca,qkcb->kab/dot_general | solution.py:72
  99.2 3.5 %convolution_bitcast_fusion.5 = f32[4,1536,48]{1,2,0:T(8,128)} fusion(bf16[4,96,1536]{2,1,0:T(8,128)(2,1)} %gather_fusion.2, pred[4]{0:T(512)(128)(4,1)S(1)} %copy-done.11, bf16[2,96,1536]{2,1,0:T(8,128)(2,1)} %copy-done.1, bf16[16,48,1536]{2,1,0:T(8,128)(2,1)S(1)} %bitcast.270, s32[]{:T(128)S(6)} %select_n.182), kind=kOutput, calls=%fused_computation.21 | convolution fusion | flops 227119104 | bytes 3244548 | tf_op jit(solution)/shard_map/qca,qkcb->kab/dot_general | solution.py:72
  102.7 3.4 %convolution_bitcast_fusion.4 = f32[4,1536,48]{1,2,0:T(8,128)} fusion(bf16[4,96,1536]{2,1,0:T(8,128)(2,1)} %gather_fusion.3, pred[4]{0:T(512)(128)(4,1)S(1)} %copy-done.10, bf16[2,96,1536]{2,1,0:T(8,128)(2,1)} %collective-permute-done.2, bf16[16,48,1536]{2,1,0:T(8,128)(2,1)S(1)} %bitcast.271, s32[]{:T(128)S(6)} %select_n.186), kind=kOutput, calls=%fused_computation.20 | convolution fusion | flops 227119104 | bytes 3244548 | tf_op jit(solution)/shard_map/qca,qkcb->kab/dot_general | solution.py:72
  106.1 3.4 %convolution_bitcast_fusion.3 = f32[4,1536,48]{1,2,0:T(8,128)} fusion(bf16[4,96,1536]{2,1,0:T(8,128)(2,1)} %gather_fusion.4, pred[4]{0:T(512)(128)(4,1)S(1)} %copy-done.7, bf16[2,96,1536]{2,1,0:T(8,128)(2,1)} %collective-permute-done.3, bf16[16,48,1536]{2,1,0:T(8,128)(2,1)S(1)} %bitcast.272, s32[]{:T(128)S(6)} %select_n.190), kind=kOutput, calls=%fused_computation.19 | convolution fusion | flops 227119104 | bytes 3244548 | tf_op jit(solution)/shard_map/qca,qkcb->kab/dot_general | solution.py:72
  110.1 2.4 %scatter_fusion = f32[6,1536,48]{1,2,0:T(8,128)S(1)} fusion(f32[6,1536,48]{1,2,0:T(8,128)S(1)} %broadcast_in_dim.13, s32[4]{0:T(128)S(1)} %copy-done.15, f32[4,1536,48]{1,2,0:T(8,128)} %convolution_bitcast_fusion.7), kind=kCustom, calls=%fused_computation.8 | custom fusion | flops 294912 | bytes 3538960 | tf_op jit(solution)/shard_map/scatter-add | solution.py:75
  112.6 2.4 %scatter_fusion.1 = f32[6,1536,48]{1,2,0:T(8,128)S(1)} fusion(f32[6,1536,48]{1,2,0:T(8,128)S(1)} %scatter_fusion, s32[4]{0:T(128)S(1)} %copy-done.16, f32[4,1536,48]{1,2,0:T(8,128)} %convolution_bitcast_fusion.6), kind=kCustom, calls=%fused_computation.9 | custom fusion | flops 294912 | bytes 3538960 | tf_op jit(solution)/shard_map/scatter-add | solution.py:75
  115.0 2.4 %scatter_fusion.2 = f32[6,1536,48]{1,2,0:T(8,128)S(1)} fusion(f32[6,1536,48]{1,2,0:T(8,128)S(1)} %scatter_fusion.1, s32[4]{0:T(128)S(1)} %copy-done.19, f32[4,1536,48]{1,2,0:T(8,128)} %convolution_bitcast_fusion.5), kind=kCustom, calls=%fused_computation.10 | custom fusion | flops 294912 | bytes 3538960 | tf_op jit(solution)/shard_map/scatter-add | solution.py:75
  117.5 2.4 %scatter_fusion.3 = f32[6,1536,48]{1,2,0:T(8,128)S(1)} fusion(f32[6,1536,48]{1,2,0:T(8,128)S(1)} %scatter_fusion.2, s32[4]{0:T(128)S(1)} %copy-done.18, f32[4,1536,48]{1,2,0:T(8,128)} %convolution_bitcast_fusion.4), kind=kCustom, calls=%fused_computation.11 | custom fusion | flops 294912 | bytes 3538960 | tf_op jit(solution)/shard_map/scatter-add | solution.py:75
  119.9 2.4 %scatter_fusion.4 = f32[6,1536,48]{1,2,0:T(8,128)S(1)} fusion(f32[6,1536,48]{1,2,0:T(8,128)S(1)} %scatter_fusion.3, s32[4]{0:T(128)S(1)} %copy-done.17, f32[4,1536,48]{1,2,0:T(8,128)} %convolution_bitcast_fusion.3), kind=kCustom, calls=%fused_computation.12 | custom fusion | flops 294912 | bytes 3538960 | tf_op jit(solution)/shard_map/scatter-add | solution.py:75
  122.3 3.5 %convolution_bitcast_fusion.2 = f32[4,1536,48]{1,2,0:T(8,128)} fusion(bf16[4,96,1536]{2,1,0:T(8,128)(2,1)} %gather_fusion.5, pred[4]{0:T(512)(128)(4,1)S(1)} %copy-done.5, bf16[2,96,1536]{2,1,0:T(8,128)(2,1)} %collective-permute-done.4, bf16[16,48,1536]{2,1,0:T(8,128)(2,1)} %bitcast.273, s32[]{:T(128)S(6)} %select_n.194), kind=kOutput, calls=%fused_computation.18 | convolution fusion | flops 227119104 | bytes 3244040 | tf_op jit(solution)/shard_map/qca,qkcb->kab/dot_general | solution.py:72
  125.9 2.4 %scatter_fusion.5 = f32[6,1536,48]{1,2,0:T(8,128)S(1)} fusion(f32[6,1536,48]{1,2,0:T(8,128)S(1)} %scatter_fusion.4, s32[4]{0:T(128)S(1)} %copy-done.14, f32[4,1536,48]{1,2,0:T(8,128)} %convolution_bitcast_fusion.2), kind=kCustom, calls=%fused_computation.13 | custom fusion | flops 294912 | bytes 3538960 | tf_op jit(solution)/shard_map/scatter-add | solution.py:75
  128.3 3.5 %convolution_bitcast_fusion.1 = f32[4,1536,48]{1,2,0:T(8,128)} fusion(bf16[4,96,1536]{2,1,0:T(8,128)(2,1)} %gather_fusion.6, pred[4]{0:T(512)(128)(4,1)S(1)} %copy-done.6, bf16[2,96,1536]{2,1,0:T(8,128)(2,1)} %collective-permute-done.5, bf16[16,48,1536]{2,1,0:T(8,128)(2,1)} %bitcast.274, s32[]{:T(128)S(6)} %select_n.198), kind=kOutput, calls=%fused_computation.17 | convolution fusion | flops 227119104 | bytes 3244040 | tf_op jit(solution)/shard_map/qca,qkcb->kab/dot_general | solution.py:72
  131.8 2.4 %scatter_fusion.6 = f32[6,1536,48]{1,2,0:T(8,128)S(1)} fusion(f32[6,1536,48]{1,2,0:T(8,128)S(1)} %scatter_fusion.5, s32[4]{0:T(128)S(1)} %copy-done.13, f32[4,1536,48]{1,2,0:T(8,128)} %convolution_bitcast_fusion.1), kind=kCustom, calls=%fused_computation.14 | custom fusion | flops 294912 | bytes 3538960 | tf_op jit(solution)/shard_map/scatter-add | solution.py:75
  134.3 3.2 %convolution_bitcast_fusion = f32[4,1536,48]{1,2,0:T(8,128)} fusion(bf16[4,96,1536]{2,1,0:T(8,128)(2,1)S(1)} %gather_fusion.7, pred[4]{0:T(512)(128)(4,1)S(1)} %copy-done.12, bf16[2,96,1536]{2,1,0:T(8,128)(2,1)} %collective-permute-done.6, bf16[16,48,1536]{2,1,0:T(8,128)(2,1)} %bitcast.275, s32[]{:T(128)S(6)} %select_n.202), kind=kOutput, calls=%fused_computation.16 | convolution fusion | flops 227119104 | bytes 3244040 | tf_op jit(solution)/shard_map/qca,qkcb->kab/dot_general | solution.py:72
  137.4 2.4 %scatter_fusion.7 = f32[6,1536,48]{1,2,0:T(8,128)S(1)} fusion(f32[6,1536,48]{1,2,0:T(8,128)S(1)} %scatter_fusion.6, s32[4]{0:T(128)S(1)} %copy-done.20, f32[4,1536,48]{1,2,0:T(8,128)} %convolution_bitcast_fusion), kind=kCustom, calls=%fused_computation.15 | custom fusion | flops 294912 | bytes 3538960 | tf_op jit(solution)/shard_map/scatter-add | solution.py:75
  141.2 41.2 %all_to_all.10 = bf16[16,6,96,48]{2,3,1,0:T(8,128)(2,1)S(1)} all-to-all(bf16[16,6,96,48]{2,3,1,0:T(8,128)(2,1)S(1)} %bitcast.277), channel_id=1, replica_groups=mesh['va_0'=2,'va_1'=8,'vb'=8,'occ'=4] {'va_0','va_1'}, dimensions={0} | all-to-all | bytes 1769472 | tf_op jit(solution)/shard_map/all_to_all | solution.py:53
  (92 shorter events, 23.7 us)
Async XLA Ops:
  6.5 33.5 %collective-permute-start = (bf16[2,96,1536]{2,1,0:T(8,128)(2,1)}, bf16[2,96,1536]{2,1,0:T(8,128)(2,1)S(1)}, u32[]{:S(2)}, u32[]{:S(2)}) collective-permute-start(bf16[2,96,1536]{2,1,0:T(8,128)(2,1)} %param.7), channel_id=1, source_target_pairs={{28,0},{0,4},{4,8},{8,12},{12,16},{16,20},{20,24},{24,28},{29,1},{... | collective-permute-start | bytes 1769480 | tf_op jit(solution)/shard_map/ppermute | solution.py:43
  11.1 41.8 %collective-permute-start.1 = (bf16[2,96,1536]{2,1,0:T(8,128)(2,1)}, bf16[2,96,1536]{2,1,0:T(8,128)(2,1)S(1)}, u32[]{:S(2)}, u32[]{:S(2)}) collective-permute-start(bf16[2,96,1536]{2,1,0:T(8,128)(2,1)} %param.7), channel_id=1, source_target_pairs={{4,0},{8,4},{12,8},{16,12},{20,16},{24,20},{28,24},{0,28},{5,1},{9... | collective-permute-start | bytes 1769480 | tf_op jit(solution)/shard_map/ppermute | solution.py:43
  15.4 4.3 %copy-start.3 = (bf16[1,48,1536]{2,1,0:T(8,128)(2,1)S(1)}, bf16[1,48,1536]{2,1,0:T(8,128)(2,1)}, u32[]{:S(2)}) copy-start(bf16[1,48,1536]{2,1,0:T(8,128)(2,1)} %param.8) | copy-start | bytes 442372
  15.4 17.3 %copy-start.4 = (s32[8,4]{0,1:T(4,128)S(1)}, s32[8,4]{0,1:T(4,128)}, u32[]{:S(2)}) copy-start(s32[8,4]{0,1:T(4,128)} %param.9) | copy-start | bytes 388
  15.4 57.4 %all-to-all-start = ((bf16[4,6,96,384]{3,2,1,0:T(8,128)(2,1)}), bf16[4,6,96,384]{3,2,1,0:T(8,128)(2,1)S(1)}, u32[]{:S(2)}, u32[]{:S(2)}) async-start(bf16[4,6,96,384]{3,2,1,0:T(8,128)(2,1)} %broadcast_in_dim.14), calls=%async_computation | async-start | bytes 3538944 | tf_op jit(solution)/shard_map/all_to_all | solution.py:12
  19.8 69.9 %all-gather.4.cloned.1.call-start = ((), (), s32[]{:S(2)}) async-start(), calls=%async_computation.2 | async-start | bytes 2654208 | tf_op jit(solution)/shard_map/all_gather | solution.py:29
  40.0 32.8 %copy-start.2 = (bf16[2,96,1536]{2,1,0:T(8,128)(2,1)}, bf16[2,96,1536]{2,1,0:T(8,128)(2,1)S(1)}, u32[]{:S(2)}) copy-start(bf16[2,96,1536]{2,1,0:T(8,128)(2,1)S(1)} %collective-permute-done) | copy-start | bytes 1769476
  40.0 21.8 %collective-permute-start.2 = (bf16[2,96,1536]{2,1,0:T(8,128)(2,1)S(1)}, bf16[2,96,1536]{2,1,0:T(8,128)(2,1)}, u32[]{:S(2)}, u32[]{:S(2)}) collective-permute-start(bf16[2,96,1536]{2,1,0:T(8,128)(2,1)S(1)} %collective-permute-done), channel_id=1, source_target_pairs={{28,0},{0,4},{4,8},{8,12},{12,16},{16,20},{20,24},{24,28},{29,1},{... | collective-permute-start | bytes 1769480 | tf_op jit(solution)/shard_map/ppermute | solution.py:43
  52.9 19.9 %copy-start.1 = (bf16[2,96,1536]{2,1,0:T(8,128)(2,1)}, bf16[2,96,1536]{2,1,0:T(8,128)(2,1)S(1)}, u32[]{:S(2)}) copy-start(bf16[2,96,1536]{2,1,0:T(8,128)(2,1)S(1)} %collective-permute-done.1) | copy-start | bytes 1769476
  52.9 17.9 %collective-permute-start.3 = (bf16[2,96,1536]{2,1,0:T(8,128)(2,1)S(1)}, bf16[2,96,1536]{2,1,0:T(8,128)(2,1)}, u32[]{:S(2)}, u32[]{:S(2)}) collective-permute-start(bf16[2,96,1536]{2,1,0:T(8,128)(2,1)S(1)} %collective-permute-done.1), channel_id=1, source_target_pairs={{4,0},{8,4},{12,8},{16,12},{20,16},{24,20},{28,24},{0,28},{5,1},{9... | collective-permute-start | bytes 1769480 | tf_op jit(solution)/shard_map/ppermute | solution.py:43
  61.8 24.0 %collective-permute-start.4 = (bf16[2,96,1536]{2,1,0:T(8,128)(2,1)}, bf16[2,96,1536]{2,1,0:T(8,128)(2,1)}, u32[]{:S(2)}, u32[]{:S(2)}) collective-permute-start(bf16[2,96,1536]{2,1,0:T(8,128)(2,1)} %collective-permute-done.2), channel_id=1, source_target_pairs={{28,0},{0,4},{4,8},{8,12},{12,16},{16,20},{20,24},{24,28},{29,1},{... | collective-permute-start | bytes 1769480 | tf_op jit(solution)/shard_map/ppermute | solution.py:43
  70.9 57.5 %collective-permute-start.5 = (bf16[2,96,1536]{2,1,0:T(8,128)(2,1)}, bf16[2,96,1536]{2,1,0:T(8,128)(2,1)}, u32[]{:S(2)}, u32[]{:S(2)}) collective-permute-start(bf16[2,96,1536]{2,1,0:T(8,128)(2,1)} %collective-permute-done.3), channel_id=1, source_target_pairs={{4,0},{8,4},{12,8},{16,12},{20,16},{24,20},{28,24},{0,28},{5,1},{9... | collective-permute-start | bytes 1769480 | tf_op jit(solution)/shard_map/ppermute | solution.py:43
  85.8 48.5 %collective-permute-start.6 = (bf16[2,96,1536]{2,1,0:T(8,128)(2,1)}, bf16[2,96,1536]{2,1,0:T(8,128)(2,1)}, u32[]{:S(2)}, u32[]{:S(2)}) collective-permute-start(bf16[2,96,1536]{2,1,0:T(8,128)(2,1)} %collective-permute-done.4), channel_id=1, source_target_pairs={{28,0},{0,4},{4,8},{8,12},{12,16},{16,20},{20,24},{24,28},{29,1},{... | collective-permute-start | bytes 1769480 | tf_op jit(solution)/shard_map/ppermute | solution.py:43
  89.6 1.9 copy-start.8
  91.5 14.6 %copy-start = (bf16[2,8,1,48,1536]{4,3,1,0,2:T(8,128)(2,1)}, bf16[2,8,1,48,1536]{4,3,1,0,2:T(8,128)(2,1)S(1)}, u32[]{:S(2)}) copy-start(bf16[2,8,1,48,1536]{4,3,1,0,2:T(8,128)(2,1)S(1)} %copy.7) | copy-start | bytes 7077892
  91.5 4.3 %copy-start.9 = (pred[4]{0:T(512)(128)(4,1)S(1)}, pred[4]{0:T(512)(128)(4,1)}, u32[]{:S(2)}) copy-start(pred[4]{0:T(512)(128)(4,1)} %compare_and_fusion.6) | copy-start | bytes 16
  95.8 3.4 %copy-start.11 = (pred[4]{0:T(512)(128)(4,1)S(1)}, pred[4]{0:T(512)(128)(4,1)}, u32[]{:S(2)}) copy-start(pred[4]{0:T(512)(128)(4,1)} %compare_and_fusion.5) | copy-start | bytes 16
  99.2 3.5 %copy-start.10 = (pred[4]{0:T(512)(128)(4,1)S(1)}, pred[4]{0:T(512)(128)(4,1)}, u32[]{:S(2)}) copy-start(pred[4]{0:T(512)(128)(4,1)} %compare_and_fusion.4) | copy-start | bytes 16
  102.7 3.4 %copy-start.7 = (pred[4]{0:T(512)(128)(4,1)S(1)}, pred[4]{0:T(512)(128)(4,1)}, u32[]{:S(2)}) copy-start(pred[4]{0:T(512)(128)(4,1)} %compare_and_fusion.3) | copy-start | bytes 16
  109.5 0.6 copy-start.15
  110.1 2.4 %copy-start.16 = (s32[4]{0:T(128)S(1)}, s32[4]{0:T(128)}, u32[]{:S(2)}) copy-start(s32[4]{0:T(128)} %fusion.177) | copy-start | bytes 52
  112.6 2.4 %copy-start.19 = (s32[4]{0:T(128)S(1)}, s32[4]{0:T(128)}, u32[]{:S(2)}) copy-start(s32[4]{0:T(128)} %fusion.178) | copy-start | bytes 52
  115.0 2.4 %copy-start.18 = (s32[4]{0:T(128)S(1)}, s32[4]{0:T(128)}, u32[]{:S(2)}) copy-start(s32[4]{0:T(128)} %fusion.179) | copy-start | bytes 52
  117.4 2.4 %copy-start.17 = (s32[4]{0:T(128)S(1)}, s32[4]{0:T(128)}, u32[]{:S(2)}) copy-start(s32[4]{0:T(128)} %fusion.180) | copy-start | bytes 52
  119.9 2.4 %copy-start.5 = (pred[4]{0:T(512)(128)(4,1)S(1)}, pred[4]{0:T(512)(128)(4,1)}, u32[]{:S(2)}) copy-start(pred[4]{0:T(512)(128)(4,1)} %compare_and_fusion.2) | copy-start | bytes 16
  122.3 3.6 %copy-start.14 = (s32[4]{0:T(128)S(1)}, s32[4]{0:T(128)}, u32[]{:S(2)}) copy-start(s32[4]{0:T(128)} %fusion.181) | copy-start | bytes 52
  125.9 2.4 %copy-start.6 = (pred[4]{0:T(512)(128)(4,1)S(1)}, pred[4]{0:T(512)(128)(4,1)}, u32[]{:S(2)}) copy-start(pred[4]{0:T(512)(128)(4,1)} %compare_and_fusion.1) | copy-start | bytes 16
  128.3 3.5 %copy-start.13 = (s32[4]{0:T(128)S(1)}, s32[4]{0:T(128)}, u32[]{:S(2)}) copy-start(s32[4]{0:T(128)} %fusion.182) | copy-start | bytes 52
  131.8 2.4 %copy-start.12 = (pred[4]{0:T(512)(128)(4,1)S(1)}, pred[4]{0:T(512)(128)(4,1)}, u32[]{:S(2)}) copy-start(pred[4]{0:T(512)(128)(4,1)} %compare_and_fusion) | copy-start | bytes 16
  134.2 3.2 %copy-start.20 = (s32[4]{0:T(128)S(1)}, s32[4]{0:T(128)}, u32[]{:S(2)}) copy-start(s32[4]{0:T(128)} %fusion.183) | copy-start | bytes 52
Sparse Core Ops, SparseCore 0:
  32.7 43.9 all-gather.3
where the time goes:
time: 191 us; the launch traced here: 190 us
  blocking collectives  54 us (28%)
  starting transfers between devices  34.1 us (18%)
  other arithmetic  31.3 us (16%)
  matrix products  28.2 us (15%)
  local copies, waits for them, and re-layouts  19.4 us (10%)
  between operations  14 us (7%)
  waiting for transfers between devices  9.3 us (5%)
    all_to_all x1, blocking collectives, sent_and_summed(): lax.all_to_all(cut_along(array, dim, devices), axis, 0, 0, tiled=True)  41.2 us
    ppermute x7, starting transfers between devices, from_behind(): return lax.ppermute(block, axis, route)  29.7 us
    dot_general x8, matrix products, contribute(): jnp.einsum('qca,qkcb->kab', bra_block, half, preferred_element_type=jnp.f...  28.2 us
    scatter-add x8, other arithmetic, contribute(): return total.at[picks].add(partial_terms)  19.3 us
    all_gather x1, blocking collectives, stacked_from(): blocks = lax.all_gather(blocks, axes[k])  12.8 us
    gather x8, local copies, waits for them, and re-layouts, contribute(): chosen = jnp.take(tau_rows, picks, axis=0)  12.7 us
    ppermute x7, waiting for transfers between devices, from_behind(): return lax.ppermute(block, axis, route)  9.26 us
    and x8, other arithmetic, contribute(): chosen = jnp.take(tau_rows, picks, axis=0)  4.42 us
  transfers between devices with their start and end apart: 9, of which 2 were waited for; matrix products, arithmetic and copies ran while one was open for 37% of the time, Pallas kernels for 0%

commit v1 on v0

v1 whole, which is shorter than its diff:
```python
import jax
import jax.numpy as jnp
from jax import lax
from jax.experimental import pallas as pl
from jax.experimental.pallas import tpu as pltpu
from jax.sharding import Mesh
from jax.sharding import PartitionSpec as P

AXES = ("zh", "y", "zl", "core", "x")
VA = ("zh", "y")
F32 = jnp.float32
BF16 = jnp.bfloat16
VMEM = pl.BlockSpec(memory_space=pltpu.VMEM)
SMEM = pl.BlockSpec(memory_space=pltpu.SMEM)
PARAMS = pltpu.CompilerParams(vmem_limit_bytes=20 << 20)


def shifted(block, axis, by):
    n = lax.axis_size(axis)
    return lax.ppermute(block, axis, [(i, (i + by) % n) for i in range(n)])


def copies_from(array, axis):
    copies = jnp.broadcast_to(array, (lax.axis_size(axis), *array.shape))
    return lax.all_to_all(copies, axis, 0, 0, tiled=True)


def half_kernel(lists, where, ket, mine, theirs, half):
    zh, zl, core = where[0], where[1], where[2]
    cols = ket.shape[1]
    parts, own, rows, width = mine.shape
    n_q = ket.shape[0]
    places = []
    for other in range(2):
        side = core if other == 0 else 1 - core
        for s in range(4):
            for j in range(2):
                places.append(4 * ((zl - s + 4) % 4) + 2 * side + j)
    lhs = []
    for q in places:
        high = q // 8
        lhs.append(ket[(q % 8) * 2 + jnp.where(high == zh, 0, 1)])
    lhs = jnp.concatenate(lhs, axis=0)
    out = None
    for x in range(parts):
        rhs = jnp.concatenate([mine[x], theirs[x]], axis=0).reshape(2 * own * rows, width)
        term = lax.dot_general(
            lhs[:, x * width : (x + 1) * width], rhs, (((1,), (1,)), ((), ())), preferred_element_type=F32
        )
        out = term if out is None else out + term
    for side in range(2):
        first = own * (core if side == 0 else 1 - core)
        for k in range(own):
            p = first + k
            at = side * own + k
            for i in range(n_q):
                group = places[i] // 2
                wanted = lists[group, 0] == p
                for m in range(1, lists.shape[1]):
                    wanted = jnp.logical_or(wanted, lists[group, m] == p)
                block = out[i * cols : (i + 1) * cols, at * rows : (at + 1) * rows]
                block = jnp.where(wanted, block, 0.0).astype(BF16)
                half[pl.ds(pl.multiple_of(p * cols, 16), cols), i * rows : (i + 1) * rows] = block


def total_kernel(half, *refs):
    bras, out = refs[:-1], refs[-1]
    rows = bras[0].shape[1]
    n_a = bras[0].shape[2]
    m = half.shape[0]
    width = 4 * rows
    keep = m * rows // 128
    lhs = half[...]
    for j in range(0, n_a, width):
        rhs = jnp.concatenate([b[i, :, j : j + width] for b in bras for i in range(b.shape[0])], axis=0)
        sums = jnp.dot(lhs, rhs, preferred_element_type=F32)
        for i in range(4):
            block = sums[:, i * rows : (i + 1) * rows]
            tail = jnp.concatenate([block[keep:, 32 * s : 32 * s + 32] for s in range(rows // 32)], axis=0)
            out[j // rows + i] = jnp.concatenate([block[:keep], tail], axis=1).astype(BF16)


def sum_kernel(parts, out):
    rows = out.shape[1]
    keep, step = parts.shape[1], out.shape[0] - parts.shape[1]
    sums = parts[0].astype(F32)
    for i in range(1, parts.shape[0]):
        sums = sums + parts[i].astype(F32)
    out[:keep, :] = sums[:, :rows]
    tail = [sums[step * s : step * (s + 1), rows:] for s in range(rows // 32)]
    out[keep:, :] = jnp.concatenate(tail, axis=1)


def per_device(amplitudes, bra_factor, ket_factor, pair_list):
    pairs, rows, width = amplitudes.shape
    cols = ket_factor.shape[1]
    n_a = bra_factor.shape[2]
    core = lax.axis_index("core")
    where = jnp.stack([lax.axis_index("zh"), lax.axis_index("zl"), core]).astype(jnp.int32)

    ket = jnp.concatenate([ket_factor, shifted(ket_factor, "zh", 1)], axis=0)
    ket = lax.all_gather(ket, "y", axis=0, tiled=True)
    bras = [bra_factor] + [shifted(bra_factor, "zl", s) for s in range(1, 4)]
    bras = bras + [shifted(b, "core", 1) for b in bras]
    mine = copies_from(lax.dynamic_slice_in_dim(amplitudes, core * (pairs // 2), pairs // 2, 0), "x")
    theirs = shifted(mine, "core", 1)

    n_q = 2 * len(bras)
    half = pl.pallas_call(
        half_kernel,
        in_specs=[SMEM, SMEM, VMEM, VMEM, VMEM],
        out_specs=VMEM,
        out_shape=jax.ShapeDtypeStruct((pairs * cols, n_q * rows), BF16),
        compiler_params=PARAMS,
        name="half",
    )(pair_list, where, ket, mine, theirs)
    n_va = n_a // rows
    total = pl.pallas_call(
        total_kernel,
        in_specs=[VMEM] * (1 + len(bras)),
        out_specs=VMEM,
        out_shape=jax.ShapeDtypeStruct((n_va, pairs * cols * rows // 128, 128), BF16),
        compiler_params=PARAMS,
        name="total",
    )(half, *bras)
    total = lax.all_to_all(total, VA, 0, 0, tiled=True)
    out = pl.pallas_call(
        sum_kernel,
        in_specs=[VMEM],
        out_specs=VMEM,
        out_shape=jax.ShapeDtypeStruct((pairs * cols, rows), F32),
        compiler_params=PARAMS,
        name="sum",
    )(total)
    return out.reshape(pairs, cols, rows).transpose(0, 2, 1)


def solution(mesh):
    torus = Mesh(mesh.devices.reshape(2, 8, 4, 2, 4), AXES)
    return jax.shard_map(
        per_device,
        mesh=torus,
        in_specs=(P(None, VA, "x"), P(("zl", "core"), VA, None), P(VA, ("zl", "core", "x"), None), P()),
        out_specs=P(None, VA, ("zl", "core", "x")),
        check_vma=False,
    )
```

time: 191 us -> 147 us (0.77)
  the two profiles are of different devices: /device:TPU:15 before, /device:TPU:74 now
where the time goes in v1:
time: 147 us; the launch traced here: 146 us
  waiting for transfers between devices  45.8 us (31%)
  blocking collectives  39.7 us (27%)
  starting transfers between devices  34.1 us (23%)
  between operations  13.6 us (9%)
  Pallas kernels  8.53 us (6%)
  local copies, waits for them, and re-layouts  2.78 us (2%)
  other arithmetic  1.72 us (1%)
    ppermute x9, waiting for transfers between devices, shifted(): return lax.ppermute(block, axis, [(i, (i + by) % n) for i in range(n)])  43.3 us
    all_to_all x1, blocking collectives, per_device(): total = lax.all_to_all(total, VA, 0, 0, tiled=True)  39.7 us
    ppermute x9, starting transfers between devices, shifted(): return lax.ppermute(block, axis, [(i, (i + by) % n) for i in range(n)])  29.3 us
    all_to_all x1, starting transfers between devices, copies_from(): return lax.all_to_all(copies, axis, 0, 0, tiled=True)  4.82 us
    pallas_call x1, Pallas kernels, per_device(): pl.pallas_call(total_kernel, in_specs=[VMEM] * (1 + len(bras)), out_specs...  4.24 us
    pallas_call x1, Pallas kernels, per_device(): pl.pallas_call(half_kernel, in_specs=[SMEM, SMEM, VMEM, VMEM, VMEM], out_...  3.44 us
  transfers between devices with their start and end apart: 11, of which 4 were waited for; matrix products, arithmetic and copies ran while one was open for 1% of the time, Pallas kernels for 2%

profile of v1, /device:TPU:74, one launch (start us, length us, event | category | flops | bytes accessed | tf_op | source)
XLA Modules:
  0.0 146.2 jit_solution(15297393550947351501)
XLA Ops:
  6.5 0.0 copy-start
  6.5 10.1 %collective-permute-start = (bf16[1,48,1536]{2,1,0:T(8,128)(2,1)}, bf16[1,48,1536]{2,1,0:T(8,128)(2,1)S(1)}, u32[]{:S(2)}, u32[]{:S(2)}) collective-permute-start(bf16[1,48,1536]{2,1,0:T(8,128)(2,1)} %param.6), channel_id=1, source_target_pairs={{0,256},{256,0},{1,257},{257,1},{2,258},{258,2},{3,259},{259,3},{4... | collective-permute-start | bytes 442376 | tf_op jit(solution)/shard_map/ppermute | solution.py:20
  16.7 7.3 %collective-permute-done = bf16[1,48,1536]{2,1,0:T(8,128)(2,1)S(1)} collective-permute-done((bf16[1,48,1536]{2,1,0:T(8,128)(2,1)}, bf16[1,48,1536]{2,1,0:T(8,128)(2,1)S(1)}, u32[]{:S(2)}, u32[]{:S(2)}) %collective-permute-start) | collective-permute-done | bytes 147488 | tf_op jit(solution)/shard_map/ppermute | solution.py:20
  24.1 1.6 %pad_maximum_fusion = bf16[2,48,1536]{2,1,0:T(8,128)(2,1)} fusion(bf16[1,48,1536]{2,1,0:T(8,128)(2,1)S(1)} %collective-permute-done, bf16[1,48,1536]{2,1,0:T(8,128)(2,1)} %param.6), kind=kLoop, calls=%fused_computation | loop fusion | flops 147456 | bytes 589824 | tf_op jit(solution)/shard_map/concatenate | solution.py:101
  25.7 0.0 all-gather.2.cloned.1.call-update
  25.8 1.0 broadcast_in_dim.3
  26.8 4.8 %all-to-all-start = ((bf16[4,3,96,384]{3,2,1,0:T(8,128)(2,1)}), bf16[4,3,96,384]{3,2,1,0:T(8,128)(2,1)S(1)}, u32[]{:S(2)}, u32[]{:S(2)}) async-start(bf16[4,3,96,384]{3,2,1,0:T(8,128)(2,1)} %broadcast_in_dim.3), calls=%async_computation | async-start | bytes 1769472 | tf_op jit(solution)/shard_map/all_to_all | solution.py:25
  31.6 0.0 copy-done.2
  31.6 3.3 %collective-permute-start.2 = (bf16[2,96,1536]{2,1,0:T(8,128)(2,1)S(1)}, bf16[2,96,1536]{2,1,0:T(8,128)(2,1)S(1)}, u32[]{:S(2)}, u32[]{:S(2)}) collective-permute-start(bf16[2,96,1536]{2,1,0:T(8,128)(2,1)S(1)} %copy-done.2), channel_id=1, source_target_pairs={{0,8},{8,16},{16,24},{24,0},{1,9},{9,17},{17,25},{25,1},{2,10},{10... | collective-permute-start | bytes 1769480 | tf_op jit(solution)/shard_map/ppermute | solution.py:20
  34.9 1.9 %collective-permute-start.3 = (bf16[2,96,1536]{2,1,0:T(8,128)(2,1)S(1)}, bf16[2,96,1536]{2,1,0:T(8,128)(2,1)}, u32[]{:S(2)}, u32[]{:S(2)}) collective-permute-start(bf16[2,96,1536]{2,1,0:T(8,128)(2,1)S(1)} %copy-done.2), channel_id=1, source_target_pairs={{0,16},{8,24},{16,0},{24,8},{1,17},{9,25},{17,1},{25,9},{2,18},{10... | collective-permute-start | bytes 1769480 | tf_op jit(solution)/shard_map/ppermute | solution.py:20
  36.8 3.4 %collective-permute-start.4 = (bf16[2,96,1536]{2,1,0:T(8,128)(2,1)S(1)}, bf16[2,96,1536]{2,1,0:T(8,128)(2,1)}, u32[]{:S(2)}, u32[]{:S(2)}) collective-permute-start(bf16[2,96,1536]{2,1,0:T(8,128)(2,1)S(1)} %copy-done.2), channel_id=1, source_target_pairs={{0,24},{8,0},{16,8},{24,16},{1,25},{9,1},{17,9},{25,17},{2,26},{10... | collective-permute-start | bytes 1769480 | tf_op jit(solution)/shard_map/ppermute | solution.py:20
  40.2 2.5 %all-to-all-done.mine = bf16[4,3,96,384]{3,2,1,0:T(8,128)(2,1)S(1)} async-done(((bf16[4,3,96,384]{3,2,1,0:T(8,128)(2,1)}), bf16[4,3,96,384]{3,2,1,0:T(8,128)(2,1)S(1)}, u32[]{:S(2)}, u32[]{:S(2)}) %all-to-all-start) | async-done | bytes 884768 | tf_op jit(solution)/shard_map/all_to_all | solution.py:25
  42.8 1.9 %collective-permute-start.1 = (bf16[4,3,96,384]{3,2,1,0:T(8,128)(2,1)S(1)}, bf16[4,3,96,384]{3,2,1,0:T(8,128)(2,1)S(1)}, u32[]{:S(2)}, u32[]{:S(2)}) collective-permute-start(bf16[4,3,96,384]{3,2,1,0:T(8,128)(2,1)S(1)} %all-to-all-done.mine), channel_id=1, source_target_pairs={{0,4},{4,0},{1,5},{5,1},{2,6},{6,2},{3,7},{7,3},{8,12},{12,8},{9,1... | collective-permute-start | bytes 2654216 | tf_op jit(solution)/shard_map/ppermute | solution.py:20
  44.7 2.4 %collective-permute-start.5 = (bf16[2,96,1536]{2,1,0:T(8,128)(2,1)S(1)}, bf16[2,96,1536]{2,1,0:T(8,128)(2,1)}, u32[]{:S(2)}, u32[]{:S(2)}) collective-permute-start(bf16[2,96,1536]{2,1,0:T(8,128)(2,1)S(1)} %copy-done.2), channel_id=1, source_target_pairs={{0,4},{4,0},{1,5},{5,1},{2,6},{6,2},{3,7},{7,3},{8,12},{12,8},{9,1... | collective-permute-start | bytes 1769480 | tf_op jit(solution)/shard_map/ppermute | solution.py:20
  47.1 26.8 %collective-permute-done.2.refs_1_ = bf16[2,96,1536]{2,1,0:T(8,128)(2,1)S(1)} collective-permute-done((bf16[2,96,1536]{2,1,0:T(8,128)(2,1)S(1)}, bf16[2,96,1536]{2,1,0:T(8,128)(2,1)S(1)}, u32[]{:S(2)}, u32[]{:S(2)}) %collective-permute-start.2) | collective-permute-done | bytes 589856 | tf_op jit(solution)/shard_map/ppermute | solution.py:20
  73.9 1.9 %collective-permute-start.6 = (bf16[2,96,1536]{2,1,0:T(8,128)(2,1)S(1)}, bf16[2,96,1536]{2,1,0:T(8,128)(2,1)}, u32[]{:S(2)}, u32[]{:S(2)}) collective-permute-start(bf16[2,96,1536]{2,1,0:T(8,128)(2,1)S(1)} %collective-permute-done.2.refs_1_), channel_id=1, source_target_pairs={{0,4},{4,0},{1,5},{5,1},{2,6},{6,2},{3,7},{7,3},{8,12},{12,8},{9,1... | collective-permute-start | bytes 1769480 | tf_op jit(solution)/shard_map/ppermute | solution.py:20
  75.8 9.1 %collective-permute-done.3.refs_2_ = bf16[2,96,1536]{2,1,0:T(8,128)(2,1)} collective-permute-done((bf16[2,96,1536]{2,1,0:T(8,128)(2,1)S(1)}, bf16[2,96,1536]{2,1,0:T(8,128)(2,1)}, u32[]{:S(2)}, u32[]{:S(2)}) %collective-permute-start.3) | collective-permute-done | bytes 589856 | tf_op jit(solution)/shard_map/ppermute | solution.py:20
  84.9 1.9 %collective-permute-start.7 = (bf16[2,96,1536]{2,1,0:T(8,128)(2,1)}, bf16[2,96,1536]{2,1,0:T(8,128)(2,1)}, u32[]{:S(2)}, u32[]{:S(2)}) collective-permute-start(bf16[2,96,1536]{2,1,0:T(8,128)(2,1)} %collective-permute-done.3.refs_2_), channel_id=1, source_target_pairs={{0,4},{4,0},{1,5},{5,1},{2,6},{6,2},{3,7},{7,3},{8,12},{12,8},{9,1... | collective-permute-start | bytes 1769480 | tf_op jit(solution)/shard_map/ppermute | solution.py:20
  86.9 0.0 collective-permute-done.4.refs_3_
  86.9 2.4 %collective-permute-start.8 = (bf16[2,96,1536]{2,1,0:T(8,128)(2,1)}, bf16[2,96,1536]{2,1,0:T(8,128)(2,1)}, u32[]{:S(2)}, u32[]{:S(2)}) collective-permute-start(bf16[2,96,1536]{2,1,0:T(8,128)(2,1)} %collective-permute-done.4.refs_3_), channel_id=1, source_target_pairs={{0,4},{4,0},{1,5},{5,1},{2,6},{6,2},{3,7},{7,3},{8,12},{12,8},{9,1... | collective-permute-start | bytes 1769480 | tf_op jit(solution)/shard_map/ppermute | solution.py:20
  89.3 0.1 copy.6.lists
  89.4 0.1 pad_add_fusion.where
  89.5 0.0 collective-permute-done.1.theirs
  89.5 1.7 %copy-done.1 = bf16[16,48,1536]{2,1,0:T(8,128)(2,1)S(1)} copy-done((bf16[16,48,1536]{2,1,0:T(8,128)(2,1)S(1)}, bf16[16,48,1536]{2,1,0:T(8,128)(2,1)}, u32[]{:S(2)}) %copy-start.1) | copy-done | bytes 2359320
  91.1 3.4 %half.1 = bf16[288,1536]{1,0:T(8,128)(2,1)S(1)} custom-call(s32[8,4]{1,0:T(8,128)S(1)} %copy.6.lists, s32[3]{0:T(128)S(1)} %pad_add_fusion.where, bf16[16,48,1536]{2,1,0:T(8,128)(2,1)S(1)} %copy-done.1, bf16[4,3,96,384]{3,2,1,0:T(8,128)(2,1)S(1)} %all-to-all-done.mine, bf16[4,3,96,384]{3,2,1,0:T(8,128)(2,1)S(1)} %collective-permute-done.1.theirs), custom_call_target="tpu_custom_call" | custom-call | tf_op jit(solution)/shard_map/half/pallas_call | solution.py:109
  94.6 0.0 collective-permute-done.5.refs_4_
  94.6 0.0 collective-permute-done.6.refs_5_
  94.6 0.0 collective-permute-done.7.refs_6_
  94.6 0.0 collective-permute-done.8.refs_7_
  94.6 4.2 %total.1 = bf16[16,216,128]{2,1,0:T(8,128)(2,1)S(1)} custom-call(bf16[288,1536]{1,0:T(8,128)(2,1)S(1)} %half.1, bf16[2,96,1536]{2,1,0:T(8,128)(2,1)S(1)} %copy-done.2, bf16[2,96,1536]{2,1,0:T(8,128)(2,1)S(1)} %collective-permute-done.2.refs_1_, bf16[2,96,1536]{2,1,0:T(8,128)(2,1)} %collective-permute-done.3.refs_2_, ...), custom_call_target="tpu_custom_call" | custom-call | tf_op jit(solution)/shard_map/total/pallas_call | solution.py:118
  98.9 39.7 %all_to_all.10.parts = bf16[16,216,128]{2,1,0:T(8,128)(2,1)S(1)} all-to-all(bf16[16,216,128]{2,1,0:T(8,128)(2,1)S(1)} %total.1), channel_id=1, replica_groups=mesh['zh'=2,'y'=8,'zl'=4,'core'=2,'x'=4] {'zh','y'}, dimensions={0} | all-to-all | bytes 1769472 | tf_op jit(solution)/shard_map/all_to_all | solution.py:126
  138.5 0.8 sum.1
  (8 shorter events, 0.0 us)
Async XLA Ops:
  6.5 19.2 %copy-start = (bf16[6,96,384]{2,1,0:T(8,128)(2,1)S(1)}, bf16[6,96,384]{2,1,0:T(8,128)(2,1)}, u32[]{:S(2)}) copy-start(bf16[6,96,384]{2,1,0:T(8,128)(2,1)} %param.4) | copy-start | bytes 1327108
  6.5 25.1 %copy-start.2 = (bf16[2,96,1536]{2,1,0:T(8,128)(2,1)S(1)}, bf16[2,96,1536]{2,1,0:T(8,128)(2,1)}, u32[]{:S(2)}) copy-start(bf16[2,96,1536]{2,1,0:T(8,128)(2,1)} %refs_0_.1) | copy-start | bytes 1769476
  6.5 82.7 %copy-start.3 = (s32[8,4]{0,1:T(4,128)S(1)}, s32[8,4]{0,1:T(4,128)}, u32[]{:S(2)}) copy-start(s32[8,4]{0,1:T(4,128)} %param.7) | copy-start | bytes 388
  6.5 82.9 %all-gather.2.cloned.1.call-start = ((), (), s32[]{:S(2)}) async-start(), calls=%async_computation.2 | async-start | bytes 2654208 | tf_op jit(solution)/shard_map/all_gather | solution.py:102
  6.5 17.5 %collective-permute-start = (bf16[1,48,1536]{2,1,0:T(8,128)(2,1)}, bf16[1,48,1536]{2,1,0:T(8,128)(2,1)S(1)}, u32[]{:S(2)}, u32[]{:S(2)}) collective-permute-start(bf16[1,48,1536]{2,1,0:T(8,128)(2,1)} %param.6), channel_id=1, source_target_pairs={{0,256},{256,0},{1,257},{257,1},{2,258},{258,2},{3,259},{259,3},{4... | collective-permute-start | bytes 442376 | tf_op jit(solution)/shard_map/ppermute | solution.py:20
  26.8 16.0 %all-to-all-start = ((bf16[4,3,96,384]{3,2,1,0:T(8,128)(2,1)}), bf16[4,3,96,384]{3,2,1,0:T(8,128)(2,1)S(1)}, u32[]{:S(2)}, u32[]{:S(2)}) async-start(bf16[4,3,96,384]{3,2,1,0:T(8,128)(2,1)} %broadcast_in_dim.3), calls=%async_computation | async-start | bytes 1769472 | tf_op jit(solution)/shard_map/all_to_all | solution.py:25
  31.6 42.3 %collective-permute-start.2 = (bf16[2,96,1536]{2,1,0:T(8,128)(2,1)S(1)}, bf16[2,96,1536]{2,1,0:T(8,128)(2,1)S(1)}, u32[]{:S(2)}, u32[]{:S(2)}) collective-permute-start(bf16[2,96,1536]{2,1,0:T(8,128)(2,1)S(1)} %copy-done.2), channel_id=1, source_target_pairs={{0,8},{8,16},{16,24},{24,0},{1,9},{9,17},{17,25},{25,1},{2,10},{10... | collective-permute-start | bytes 1769480 | tf_op jit(solution)/shard_map/ppermute | solution.py:20
  34.9 50.0 %collective-permute-start.3 = (bf16[2,96,1536]{2,1,0:T(8,128)(2,1)S(1)}, bf16[2,96,1536]{2,1,0:T(8,128)(2,1)}, u32[]{:S(2)}, u32[]{:S(2)}) collective-permute-start(bf16[2,96,1536]{2,1,0:T(8,128)(2,1)S(1)} %copy-done.2), channel_id=1, source_target_pairs={{0,16},{8,24},{16,0},{24,8},{1,17},{9,25},{17,1},{25,9},{2,18},{10... | collective-permute-start | bytes 1769480 | tf_op jit(solution)/shard_map/ppermute | solution.py:20
  36.8 50.0 %collective-permute-start.4 = (bf16[2,96,1536]{2,1,0:T(8,128)(2,1)S(1)}, bf16[2,96,1536]{2,1,0:T(8,128)(2,1)}, u32[]{:S(2)}, u32[]{:S(2)}) collective-permute-start(bf16[2,96,1536]{2,1,0:T(8,128)(2,1)S(1)} %copy-done.2), channel_id=1, source_target_pairs={{0,24},{8,0},{16,8},{24,16},{1,25},{9,1},{17,9},{25,17},{2,26},{10... | collective-permute-start | bytes 1769480 | tf_op jit(solution)/shard_map/ppermute | solution.py:20
  42.8 46.7 %collective-permute-start.1 = (bf16[4,3,96,384]{3,2,1,0:T(8,128)(2,1)S(1)}, bf16[4,3,96,384]{3,2,1,0:T(8,128)(2,1)S(1)}, u32[]{:S(2)}, u32[]{:S(2)}) collective-permute-start(bf16[4,3,96,384]{3,2,1,0:T(8,128)(2,1)S(1)} %all-to-all-done.mine), channel_id=1, source_target_pairs={{0,4},{4,0},{1,5},{5,1},{2,6},{6,2},{3,7},{7,3},{8,12},{12,8},{9,1... | collective-permute-start | bytes 2654216 | tf_op jit(solution)/shard_map/ppermute | solution.py:20
  44.7 49.9 %collective-permute-start.5 = (bf16[2,96,1536]{2,1,0:T(8,128)(2,1)S(1)}, bf16[2,96,1536]{2,1,0:T(8,128)(2,1)}, u32[]{:S(2)}, u32[]{:S(2)}) collective-permute-start(bf16[2,96,1536]{2,1,0:T(8,128)(2,1)S(1)} %copy-done.2), channel_id=1, source_target_pairs={{0,4},{4,0},{1,5},{5,1},{2,6},{6,2},{3,7},{7,3},{8,12},{12,8},{9,1... | collective-permute-start | bytes 1769480 | tf_op jit(solution)/shard_map/ppermute | solution.py:20
  73.9 20.7 %collective-permute-start.6 = (bf16[2,96,1536]{2,1,0:T(8,128)(2,1)S(1)}, bf16[2,96,1536]{2,1,0:T(8,128)(2,1)}, u32[]{:S(2)}, u32[]{:S(2)}) collective-permute-start(bf16[2,96,1536]{2,1,0:T(8,128)(2,1)S(1)} %collective-permute-done.2.refs_1_), channel_id=1, source_target_pairs={{0,4},{4,0},{1,5},{5,1},{2,6},{6,2},{3,7},{7,3},{8,12},{12,8},{9,1... | collective-permute-start | bytes 1769480 | tf_op jit(solution)/shard_map/ppermute | solution.py:20
  84.9 9.7 %collective-permute-start.7 = (bf16[2,96,1536]{2,1,0:T(8,128)(2,1)}, bf16[2,96,1536]{2,1,0:T(8,128)(2,1)}, u32[]{:S(2)}, u32[]{:S(2)}) collective-permute-start(bf16[2,96,1536]{2,1,0:T(8,128)(2,1)} %collective-permute-done.3.refs_2_), channel_id=1, source_target_pairs={{0,4},{4,0},{1,5},{5,1},{2,6},{6,2},{3,7},{7,3},{8,12},{12,8},{9,1... | collective-permute-start | bytes 1769480 | tf_op jit(solution)/shard_map/ppermute | solution.py:20
  86.9 7.7 %collective-permute-start.8 = (bf16[2,96,1536]{2,1,0:T(8,128)(2,1)}, bf16[2,96,1536]{2,1,0:T(8,128)(2,1)}, u32[]{:S(2)}, u32[]{:S(2)}) collective-permute-start(bf16[2,96,1536]{2,1,0:T(8,128)(2,1)} %collective-permute-done.4.refs_3_), channel_id=1, source_target_pairs={{0,4},{4,0},{1,5},{5,1},{2,6},{6,2},{3,7},{7,3},{8,12},{12,8},{9,1... | collective-permute-start | bytes 1769480 | tf_op jit(solution)/shard_map/ppermute | solution.py:20
  89.5 1.7 %copy-start.1 = (bf16[16,48,1536]{2,1,0:T(8,128)(2,1)S(1)}, bf16[16,48,1536]{2,1,0:T(8,128)(2,1)}, u32[]{:S(2)}) copy-start(bf16[16,48,1536]{2,1,0:T(8,128)(2,1)} %all-gather.2.cloned.1.call-done.ket) | copy-start | bytes 7077892
Sparse Core Ops, SparseCore 0:
  25.8 44.4 all-gather.1

commit v2 on v1

v2 whole, which is shorter than its diff:
```python
import jax
import jax.numpy as jnp
from jax import lax
from jax.experimental import pallas as pl
from jax.experimental.pallas import tpu as pltpu
from jax.sharding import Mesh
from jax.sharding import PartitionSpec as P

AXES = ("zh", "y4", "y0", "zl", "core", "x")
VA = ("zh", "y4", "y0")
F32 = jnp.float32
BF16 = jnp.bfloat16
VMEM = pl.BlockSpec(memory_space=pltpu.VMEM)
SMEM = pl.BlockSpec(memory_space=pltpu.SMEM)
PARAMS = pltpu.CompilerParams(vmem_limit_bytes=20 << 20)
DIRECT = 512


def shifted(block, axis, by):
    n = lax.axis_size(axis)
    return lax.ppermute(block, axis, [(i, (i + by) % n) for i in range(n)])


def copies_from(array, axis):
    copies = jnp.broadcast_to(array, (lax.axis_size(axis), *array.shape))
    return lax.all_to_all(copies, axis, 0, 0, tiled=True)


def half_kernel(lists, where, *refs):
    kets, (mine, theirs, half, ket) = refs[:4], refs[4:]
    zh, y4, y0, _, core, x = [where[i] for i in range(6)]
    _, cols, _ = kets[0].shape
    parts, blocks, own, rows, width = mine.shape
    for s in range(4):
        for h in range(2):
            ket[2 * s + h] = kets[s][h]
    places, groups = [], []
    for r in range(2):
        side = core if r == 0 else 1 - core
        for z in range(4):
            q = 4 * z + 2 * side + y0
            high = q // 8
            s = (y4 - (q % 8) // 2 + 4) % 4
            places.append(2 * s + jnp.where(high == zh, 0, 1))
            groups.append(q // 2)
    n_q = len(places)
    out = None
    for s in range(parts):
        at = pl.multiple_of(((x - s + 4) % 4) * width, 128)
        lhs = jnp.concatenate([ket[q, :, pl.ds(at, width)] for q in places], axis=0)
        rhs = jnp.concatenate([mine[s], theirs[s]], axis=0).reshape(2 * blocks * own * rows, width)
        term = lax.dot_general(lhs, rhs, (((1,), (1,)), ((), ())), preferred_element_type=F32)
        out = term if out is None else out + term
    for side in range(2):
        first = own * (core if side == 0 else 1 - core)
        for k in range(own):
            p = first + k
            for i in range(n_q):
                wanted = lists[groups[i], 0] == p
                for m in range(1, lists.shape[1]):
                    wanted = jnp.logical_or(wanted, lists[groups[i], m] == p)
                for b in range(blocks):
                    at = ((side * blocks + b) * own + k) * rows
                    block = out[i * cols : (i + 1) * cols, at : at + rows]
                    block = jnp.where(wanted, block, 0.0).astype(BF16)
                    to = (i * blocks + b) * rows
                    half[pl.ds(pl.multiple_of(p * cols, 16), cols), to : to + rows] = block


def total_kernel(where, half, direct, direct_other, shared, shared_other, out):
    zl = where[3]
    rows = direct.shape[2]
    n_direct, n_shared = direct.shape[3], shared.shape[4]
    n_a = n_direct + shared.shape[0] * n_shared
    m = half.shape[0]
    width = 4 * rows
    keep = m * rows // 128
    lhs = half[...]

    def column(side, z, b, start):
        ref = (direct, direct_other)[side] if start < n_direct else (shared, shared_other)[side]
        if start < n_direct:
            return ref[(zl - z + 4) % 4, b, :, start : start + 128]
        x, at = divmod(start - n_direct, n_shared)
        return ref[x, z, b, :, at : at + 128]

    for j in range(0, n_a, width):
        rhs = jnp.concatenate(
            [
                jnp.concatenate([column(side, z, b, t) for t in range(j, j + width, 128)], axis=1)
                for side in range(2)
                for z in range(4)
                for b in range(2)
            ],
            axis=0,
        )
        sums = jnp.dot(lhs, rhs, preferred_element_type=F32)
        for i in range(4):
            block = sums[:, i * rows : (i + 1) * rows]
            tail = jnp.concatenate([block[keep:, 32 * s : 32 * s + 32] for s in range(rows // 32)], axis=0)
            out[j // rows + i] = jnp.concatenate([block[:keep], tail], axis=1).astype(BF16)


def sum_kernel(parts, out):
    rows = out.shape[1]
    keep, step = parts.shape[1], out.shape[0] - parts.shape[1]
    sums = parts[0].astype(F32)
    for i in range(1, parts.shape[0]):
        sums = sums + parts[i].astype(F32)
    out[:keep, :] = sums[:, :rows]
    tail = [sums[step * s : step * (s + 1), rows:] for s in range(rows // 32)]
    out[keep:, :] = jnp.concatenate(tail, axis=1)


def per_device(amplitudes, bra_factor, ket_factor, pair_list):
    pairs, rows, _ = amplitudes.shape
    cols = ket_factor.shape[1]
    n_a = bra_factor.shape[2]
    core = lax.axis_index("core")
    y0 = lax.axis_index("y0")
    x = lax.axis_index("x")
    where = jnp.stack([lax.axis_index(name) for name in AXES]).astype(jnp.int32)
    n_shared = (n_a - DIRECT) // 4

    ket_other = shifted(ket_factor, "zh", 1)

    def bra_of(parity):
        straight = lax.dynamic_slice(bra_factor, (parity, 0, 0), (1, rows, DIRECT))
        quarter = lax.dynamic_slice(bra_factor, (parity, 0, DIRECT + n_shared * x), (1, rows, n_shared))
        return jnp.concatenate([straight, quarter], axis=2)

    bra = jnp.concatenate([bra_of(y0), shifted(bra_of(1 - y0), "y0", 1)], axis=0)
    tau = lax.dynamic_slice_in_dim(amplitudes, core * (pairs // 2), pairs // 2, 0)
    tau = jnp.stack([tau, shifted(tau, "y0", 1)])
    shared = copies_from(bra[:, :, DIRECT:], "zl")
    shared = copies_from(shared, "x")
    mine = jnp.stack([tau] + [shifted(tau, "x", s) for s in range(1, 4)])
    ket = jnp.concatenate([ket_factor, ket_other], axis=0)
    kets = [ket] + [shifted(ket, "y4", s) for s in range(1, 4)]
    direct = bra[:, :, :DIRECT]
    direct = jnp.stack([direct] + [shifted(direct, "zl", s) for s in range(1, 4)])
    theirs = shifted(mine, "core", 1)
    direct_other = shifted(direct, "core", 1)
    shared_other = shifted(shared, "core", 1)

    n_q = 8
    half = pl.pallas_call(
        half_kernel,
        in_specs=[SMEM, SMEM] + [VMEM] * 6,
        out_specs=VMEM,
        out_shape=jax.ShapeDtypeStruct((pairs * cols, n_q * 2 * rows), BF16),
        scratch_shapes=[pltpu.VMEM((n_q, cols, ket.shape[2]), BF16)],
        compiler_params=PARAMS,
        name="half",
    )(pair_list, where, *kets, mine, theirs)
    n_va = n_a // rows
    total = pl.pallas_call(
        total_kernel,
        in_specs=[SMEM] + [VMEM] * 5,
        out_specs=VMEM,
        out_shape=jax.ShapeDtypeStruct((n_va, pairs * cols * rows // 128, 128), BF16),
        compiler_params=PARAMS,
        name="total",
    )(where, half, direct, direct_other, shared, shared_other)
    total = lax.all_to_all(total, VA, 0, 0, tiled=True)
    out = pl.pallas_call(
        sum_kernel,
        in_specs=[VMEM],
        out_specs=VMEM,
        out_shape=jax.ShapeDtypeStruct((pairs * cols, rows), F32),
        compiler_params=PARAMS,
        name="sum",
    )(total)
    return out.reshape(pairs, cols, rows).transpose(0, 2, 1)


def solution(mesh):
    torus = Mesh(mesh.devices.reshape(2, 4, 2, 4, 2, 4), AXES)
    return jax.shard_map(
        per_device,
        mesh=torus,
        in_specs=(P(None, VA, "x"), P(("zl", "core"), VA, None), P(VA, ("zl", "core", "x"), None), P()),
        out_specs=P(None, VA, ("zl", "core", "x")),
        check_vma=False,
    )
```

time: 147 us -> 194 us (1.32)
  the two profiles are of different devices: /device:TPU:74 before, /device:TPU:64 now
where the time goes in v2:
time: 194 us; the launch traced here: 193 us
  starting transfers between devices  71.1 us (37%)
  waiting for transfers between devices  62.9 us (32%)
  blocking collectives  43.1 us (22%)
  Pallas kernels  9.43 us (5%)
  local copies, waits for them, and re-layouts  5.93 us (3%)
    ppermute x15, starting transfers between devices, shifted(): return lax.ppermute(block, axis, [(i, (i + by) % n) for i in range(n)])  58.8 us
    ppermute x15, waiting for transfers between devices, shifted(): return lax.ppermute(block, axis, [(i, (i + by) % n) for i in range(n)])  55.5 us
    all_to_all x1, blocking collectives, per_device(): total = lax.all_to_all(total, VA, 0, 0, tiled=True)  43.1 us
    all_to_all x2, starting transfers between devices, copies_from(): return lax.all_to_all(copies, axis, 0, 0, tiled=True)  12.3 us
    all_to_all x2, waiting for transfers between devices, copies_from(): return lax.all_to_all(copies, axis, 0, 0, tiled=True)  7.38 us
    pallas_call x1, Pallas kernels, per_device(): pl.pallas_call(total_kernel, in_specs=[SMEM] + [VMEM] * 5, out_specs=VMEM...  4.45 us
    pallas_call x1, Pallas kernels, per_device(): pl.pallas_call(half_kernel, in_specs=[SMEM, SMEM] + [VMEM] * 6, out_specs...  4.13 us
  transfers between devices with their start and end apart: 17, of which 11 were waited for; matrix products, arithmetic and copies ran while one was open for 0% of the time, Pallas kernels for 2%

profile of v2, /device:TPU:64, one launch (start us, length us, event | category | flops | bytes accessed | tf_op | source)
XLA Modules:
  0.0 193.3 jit_solution(7885391935363288760)
XLA Ops:
  0.0 1.0 constant_dynamic-slice_fusion.3
  1.9 3.5 %collective-permute-start.9 = (bf16[1,96,768]{2,1,0:T(8,128)(2,1)S(1)}, bf16[1,96,768]{2,1,0:T(8,128)(2,1)S(1)}, u32[]{:S(2)}, u32[]{:S(2)}) collective-permute-start(bf16[1,96,768]{2,1,0:T(8,128)(2,1)S(1)} %pad_maximum_fusion.4), channel_id=1, source_target_pairs={{0,32},{32,0},{1,33},{33,1},{2,34},{34,2},{3,35},{35,3},{4,36},{36... | collective-permute-start | bytes 442376 | tf_op jit(solution)/shard_map/ppermute | solution.py:21
  5.4 4.0 %collective-permute-done.9 = bf16[1,96,768]{2,1,0:T(8,128)(2,1)S(1)} collective-permute-done((bf16[1,96,768]{2,1,0:T(8,128)(2,1)S(1)}, bf16[1,96,768]{2,1,0:T(8,128)(2,1)S(1)}, u32[]{:S(2)}, u32[]{:S(2)}) %collective-permute-start.9) | collective-permute-done | bytes 147488 | tf_op jit(solution)/shard_map/ppermute | solution.py:21
  10.1 8.0 %all-to-all-start = ((bf16[4,2,96,256]{3,2,1,0:T(8,128)(2,1)}), bf16[4,2,96,256]{3,2,1,0:T(8,128)(2,1)S(1)}, u32[]{:S(2)}, u32[]{:S(2)}) async-start(bf16[4,2,96,256]{3,2,1,0:T(8,128)(2,1)} %broadcast_in_dim.6), calls=%async_computation | async-start | bytes 786432 | tf_op jit(solution)/shard_map/all_to_all | solution.py:26
  18.1 7.4 %all-to-all-done = bf16[4,2,96,256]{3,2,1,0:T(8,128)(2,1)S(1)} async-done(((bf16[4,2,96,256]{3,2,1,0:T(8,128)(2,1)}), bf16[4,2,96,256]{3,2,1,0:T(8,128)(2,1)S(1)}, u32[]{:S(2)}, u32[]{:S(2)}) %all-to-all-start) | async-done | bytes 393248 | tf_op jit(solution)/shard_map/all_to_all | solution.py:26
  25.5 1.3 broadcast_in_dim.7
  26.8 4.3 %all-to-all-start.1 = ((bf16[4,4,2,96,256]{4,3,2,1,0:T(8,128)(2,1)}), bf16[4,4,2,96,256]{4,3,2,1,0:T(8,128)(2,1)}, u32[]{:S(2)}, u32[]{:S(2)}) async-start(bf16[4,4,2,96,256]{4,3,2,1,0:T(8,128)(2,1)} %broadcast_in_dim.7), calls=%async_computation.1 | async-start | bytes 3145728 | tf_op jit(solution)/shard_map/all_to_all | solution.py:26
  31.2 3.4 %collective-permute-start.4 = (bf16[3,96,384]{2,1,0:T(8,128)(2,1)S(1)}, bf16[3,96,384]{2,1,0:T(8,128)(2,1)S(1)}, u32[]{:S(2)}, u32[]{:S(2)}) collective-permute-start(bf16[3,96,384]{2,1,0:T(8,128)(2,1)S(1)} %constant_dynamic-slice_fusion.4), channel_id=1, source_target_pairs={{0,32},{32,0},{1,33},{33,1},{2,34},{34,2},{3,35},{35,3},{4,36},{36... | collective-permute-start | bytes 663560 | tf_op jit(solution)/shard_map/ppermute | solution.py:21
  34.7 4.4 %collective-permute-done.4 = bf16[3,96,384]{2,1,0:T(8,128)(2,1)S(1)} collective-permute-done((bf16[3,96,384]{2,1,0:T(8,128)(2,1)S(1)}, bf16[3,96,384]{2,1,0:T(8,128)(2,1)S(1)}, u32[]{:S(2)}, u32[]{:S(2)}) %collective-permute-start.4) | collective-permute-done | bytes 221216 | tf_op jit(solution)/shard_map/ppermute | solution.py:21
  39.1 5.4 %collective-permute-start.6 = (bf16[2,3,96,384]{3,2,1,0:T(8,128)(2,1)S(1)}, bf16[2,3,96,384]{3,2,1,0:T(8,128)(2,1)S(1)}, u32[]{:S(2)}, u32[]{:S(2)}) collective-permute-start(bf16[2,3,96,384]{3,2,1,0:T(8,128)(2,1)S(1)} %get-tuple-element.10), channel_id=1, source_target_pairs={{0,2},{1,3},{2,0},{3,1},{4,6},{5,7},{6,4},{7,5},{8,10},{9,11},{10,... | collective-permute-start | bytes 1327112 | tf_op jit(solution)/shard_map/ppermute | solution.py:21
  44.5 3.1 %collective-permute-start.7 = (bf16[2,3,96,384]{3,2,1,0:T(8,128)(2,1)S(1)}, bf16[2,3,96,384]{3,2,1,0:T(8,128)(2,1)S(1)}, u32[]{:S(2)}, u32[]{:S(2)}) collective-permute-start(bf16[2,3,96,384]{3,2,1,0:T(8,128)(2,1)S(1)} %get-tuple-element.10), channel_id=1, source_target_pairs={{0,3},{1,0},{2,1},{3,2},{4,7},{5,4},{6,5},{7,6},{8,11},{9,8},{10,9... | collective-permute-start | bytes 1327112 | tf_op jit(solution)/shard_map/ppermute | solution.py:21
  47.6 2.8 %collective-permute-start.5 = (bf16[2,3,96,384]{3,2,1,0:T(8,128)(2,1)S(1)}, bf16[2,3,96,384]{3,2,1,0:T(8,128)(2,1)S(1)}, u32[]{:S(2)}, u32[]{:S(2)}) collective-permute-start(bf16[2,3,96,384]{3,2,1,0:T(8,128)(2,1)S(1)} %get-tuple-element.10), channel_id=1, source_target_pairs={{0,1},{1,2},{2,3},{3,0},{4,5},{5,6},{6,7},{7,4},{8,9},{9,10},{10,1... | collective-permute-start | bytes 1327112 | tf_op jit(solution)/shard_map/ppermute | solution.py:21
  50.4 12.4 %collective-permute-done.6 = bf16[2,3,96,384]{3,2,1,0:T(8,128)(2,1)S(1)} collective-permute-done((bf16[2,3,96,384]{3,2,1,0:T(8,128)(2,1)S(1)}, bf16[2,3,96,384]{3,2,1,0:T(8,128)(2,1)S(1)}, u32[]{:S(2)}, u32[]{:S(2)}) %collective-permute-start.6) | collective-permute-done | bytes 442400 | tf_op jit(solution)/shard_map/ppermute | solution.py:21
  62.8 5.0 %collective-permute-done.7 = bf16[2,3,96,384]{3,2,1,0:T(8,128)(2,1)S(1)} collective-permute-done((bf16[2,3,96,384]{3,2,1,0:T(8,128)(2,1)S(1)}, bf16[2,3,96,384]{3,2,1,0:T(8,128)(2,1)S(1)}, u32[]{:S(2)}, u32[]{:S(2)}) %collective-permute-start.7) | collective-permute-done | bytes 442400 | tf_op jit(solution)/shard_map/ppermute | solution.py:21
  67.8 1.5 collective-permute-done.5
  69.5 1.9 collective-permute-start.8
  71.5 2.4 %collective-permute-start.14 = (bf16[4,4,2,96,256]{4,3,2,1,0:T(8,128)(2,1)}, bf16[4,4,2,96,256]{4,3,2,1,0:T(8,128)(2,1)}, u32[]{:S(2)}, u32[]{:S(2)}) collective-permute-start(bf16[4,4,2,96,256]{4,3,2,1,0:T(8,128)(2,1)} %all-to-all-done.1.shared), channel_id=1, source_target_pairs={{0,4},{4,0},{1,5},{5,1},{2,6},{6,2},{3,7},{7,3},{8,12},{12,8},{9,1... | collective-permute-start | bytes 4718600 | tf_op jit(solution)/shard_map/ppermute | solution.py:21
  73.9 2.1 %collective-permute-start.10 = (bf16[2,96,512]{2,1,0:T(8,128)(2,1)S(1)}, bf16[2,96,512]{2,1,0:T(8,128)(2,1)S(1)}, u32[]{:S(2)}, u32[]{:S(2)}) collective-permute-start(bf16[2,96,512]{2,1,0:T(8,128)(2,1)S(1)} %get-tuple-element.12), channel_id=1, source_target_pairs={{0,8},{8,16},{16,24},{24,0},{1,9},{9,17},{17,25},{25,1},{2,10},{10... | collective-permute-start | bytes 589832 | tf_op jit(solution)/shard_map/ppermute | solution.py:21
  76.1 8.4 %collective-permute-start = (bf16[1,48,1536]{2,1,0:T(8,128)(2,1)S(1)}, bf16[1,48,1536]{2,1,0:T(8,128)(2,1)S(1)}, u32[]{:S(2)}, u32[]{:S(2)}) collective-permute-start(bf16[1,48,1536]{2,1,0:T(8,128)(2,1)S(1)} %copy-done.3), channel_id=1, source_target_pairs={{0,256},{256,0},{1,257},{257,1},{2,258},{258,2},{3,259},{259,3},{4... | collective-permute-start | bytes 442376 | tf_op jit(solution)/shard_map/ppermute | solution.py:21
  84.5 5.8 %collective-permute-start.11 = (bf16[2,96,512]{2,1,0:T(8,128)(2,1)S(1)}, bf16[2,96,512]{2,1,0:T(8,128)(2,1)S(1)}, u32[]{:S(2)}, u32[]{:S(2)}) collective-permute-start(bf16[2,96,512]{2,1,0:T(8,128)(2,1)S(1)} %get-tuple-element.12), channel_id=1, source_target_pairs={{0,16},{8,24},{16,0},{24,8},{1,17},{9,25},{17,1},{25,9},{2,18},{10... | collective-permute-start | bytes 589832 | tf_op jit(solution)/shard_map/ppermute | solution.py:21
  90.3 2.8 %collective-permute-start.12 = (bf16[2,96,512]{2,1,0:T(8,128)(2,1)S(1)}, bf16[2,96,512]{2,1,0:T(8,128)(2,1)S(1)}, u32[]{:S(2)}, u32[]{:S(2)}) collective-permute-start(bf16[2,96,512]{2,1,0:T(8,128)(2,1)S(1)} %get-tuple-element.12), channel_id=1, source_target_pairs={{0,24},{8,0},{16,8},{24,16},{1,25},{9,1},{17,9},{25,17},{2,26},{10... | collective-permute-start | bytes 589832 | tf_op jit(solution)/shard_map/ppermute | solution.py:21
  93.1 12.3 %collective-permute-done.11 = bf16[2,96,512]{2,1,0:T(8,128)(2,1)S(1)} collective-permute-done((bf16[2,96,512]{2,1,0:T(8,128)(2,1)S(1)}, bf16[2,96,512]{2,1,0:T(8,128)(2,1)S(1)}, u32[]{:S(2)}, u32[]{:S(2)}) %collective-permute-start.11) | collective-permute-done | bytes 196640 | tf_op jit(solution)/shard_map/ppermute | solution.py:21
  106.4 1.9 collective-permute-start.13
  108.3 4.5 %collective-permute-start.1 = (bf16[2,48,1536]{2,1,0:T(8,128)(2,1)S(1)}, bf16[2,48,1536]{2,1,0:T(8,128)(2,1)S(1)}, u32[]{:S(2)}, u32[]{:S(2)}) collective-permute-start(bf16[2,48,1536]{2,1,0:T(8,128)(2,1)S(1)} %constant_dynamic-update-slice_fusion.refs_0_), channel_id=1, source_target_pairs={{0,64},{64,128},{128,192},{192,0},{1,65},{65,129},{129,193},{193,1... | collective-permute-start | bytes 884744 | tf_op jit(solution)/shard_map/ppermute | solution.py:21
  112.8 5.9 %collective-permute-start.2 = (bf16[2,48,1536]{2,1,0:T(8,128)(2,1)S(1)}, bf16[2,48,1536]{2,1,0:T(8,128)(2,1)}, u32[]{:S(2)}, u32[]{:S(2)}) collective-permute-start(bf16[2,48,1536]{2,1,0:T(8,128)(2,1)S(1)} %constant_dynamic-update-slice_fusion.refs_0_), channel_id=1, source_target_pairs={{0,128},{64,192},{128,0},{192,64},{1,129},{65,193},{129,1},{193,65... | collective-permute-start | bytes 884744 | tf_op jit(solution)/shard_map/ppermute | solution.py:21
  118.8 7.7 %collective-permute-done.1.refs_1_ = bf16[2,48,1536]{2,1,0:T(8,128)(2,1)S(1)} collective-permute-done((bf16[2,48,1536]{2,1,0:T(8,128)(2,1)S(1)}, bf16[2,48,1536]{2,1,0:T(8,128)(2,1)S(1)}, u32[]{:S(2)}, u32[]{:S(2)}) %collective-permute-start.1) | collective-permute-done | bytes 294944 | tf_op jit(solution)/shard_map/ppermute | solution.py:21
  127.2 4.9 %collective-permute-start.3 = (bf16[2,48,1536]{2,1,0:T(8,128)(2,1)S(1)}, bf16[2,48,1536]{2,1,0:T(8,128)(2,1)}, u32[]{:S(2)}, u32[]{:S(2)}) collective-permute-start(bf16[2,48,1536]{2,1,0:T(8,128)(2,1)S(1)} %constant_dynamic-update-slice_fusion.refs_0_), channel_id=1, source_target_pairs={{0,192},{64,0},{128,64},{192,128},{1,193},{65,1},{129,65},{193,129... | collective-permute-start | bytes 884744 | tf_op jit(solution)/shard_map/ppermute | solution.py:21
  132.3 5.1 %collective-permute-done.2.refs_2_ = bf16[2,48,1536]{2,1,0:T(8,128)(2,1)} collective-permute-done((bf16[2,48,1536]{2,1,0:T(8,128)(2,1)S(1)}, bf16[2,48,1536]{2,1,0:T(8,128)(2,1)}, u32[]{:S(2)}, u32[]{:S(2)}) %collective-permute-start.2) | collective-permute-done | bytes 294944 | tf_op jit(solution)/shard_map/ppermute | solution.py:21
  137.3 2.4 %collective-permute-done.3.refs_3_ = bf16[2,48,1536]{2,1,0:T(8,128)(2,1)} collective-permute-done((bf16[2,48,1536]{2,1,0:T(8,128)(2,1)S(1)}, bf16[2,48,1536]{2,1,0:T(8,128)(2,1)}, u32[]{:S(2)}, u32[]{:S(2)}) %collective-permute-start.3) | collective-permute-done | bytes 294944 | tf_op jit(solution)/shard_map/ppermute | solution.py:21
  140.7 4.1 %half.1 = bf16[288,1536]{1,0:T(8,128)(2,1)S(1)} custom-call(s32[8,4]{1,0:T(8,128)S(1)} %copy.5.lists, s32[6]{0:T(128)S(1)} %stack.66.where, bf16[2,48,1536]{2,1,0:T(8,128)(2,1)S(1)} %constant_dynamic-update-slice_fusion.refs_0_, bf16[2,48,1536]{2,1,0:T(8,128)(2,1)S(1)} %copy-done.2, bf16[2,48,1536]{2,1,0:T(8,128)(2,1)} %collective-permute-done.2.refs_2_, ...), custom_call_target="tpu_custom_call" | custom-call | tf_op jit(solution)/shard_map/half/pallas_call | solution.py:147
  144.8 4.4 %total.1 = bf16[16,216,128]{2,1,0:T(8,128)(2,1)S(1)} custom-call(s32[6]{0:T(128)S(1)} %stack.66.where, bf16[288,1536]{1,0:T(8,128)(2,1)S(1)} %half.1, bf16[4,2,96,512]{3,2,1,0:T(8,128)(2,1)S(1)} %pad_maximum_fusion.1.direct, bf16[4,2,96,512]{3,2,1,0:T(8,128)(2,1)} %collective-permute-done.13.direct_other, bf16[4,4,2,96,256]{4,3,2,1,0:T(8,128)(2,1)} %all-to-all-done.1.shared, ...), custom_call_target="tpu_custom_call" | custom-call | tf_op jit(solution)/shard_map/total/pallas_call | solution.py:157
  149.3 43.1 %all_to_all.15.parts = bf16[16,216,128]{2,1,0:T(8,128)(2,1)S(1)} all-to-all(bf16[16,216,128]{2,1,0:T(8,128)(2,1)S(1)} %total.1), channel_id=1, replica_groups=mesh['zh'=2,'y4'=4,'y0'=2,'zl'=4,'core'=2,'x'=4] {'zh','y4','y0'}, dimensions={0} | all-to-all | bytes 1769472 | tf_op jit(solution)/shard_map/all_to_all | solution.py:165
  (33 shorter events, 5.8 us)
Async XLA Ops:
  0.0 31.2 %copy-start = (bf16[6,96,384]{2,1,0:T(8,128)(2,1)S(1)}, bf16[6,96,384]{2,1,0:T(8,128)(2,1)}, u32[]{:S(2)}) copy-start(bf16[6,96,384]{2,1,0:T(8,128)(2,1)} %param.4) | copy-start | bytes 1327108
  1.9 7.5 %collective-permute-start.9 = (bf16[1,96,768]{2,1,0:T(8,128)(2,1)S(1)}, bf16[1,96,768]{2,1,0:T(8,128)(2,1)S(1)}, u32[]{:S(2)}, u32[]{:S(2)}) collective-permute-start(bf16[1,96,768]{2,1,0:T(8,128)(2,1)S(1)} %pad_maximum_fusion.4), channel_id=1, source_target_pairs={{0,32},{32,0},{1,33},{33,1},{2,34},{34,2},{3,35},{35,3},{4,36},{36... | collective-permute-start | bytes 442376 | tf_op jit(solution)/shard_map/ppermute | solution.py:21
  10.1 15.4 %all-to-all-start = ((bf16[4,2,96,256]{3,2,1,0:T(8,128)(2,1)}), bf16[4,2,96,256]{3,2,1,0:T(8,128)(2,1)S(1)}, u32[]{:S(2)}, u32[]{:S(2)}) async-start(bf16[4,2,96,256]{3,2,1,0:T(8,128)(2,1)} %broadcast_in_dim.6), calls=%async_computation | async-start | bytes 786432 | tf_op jit(solution)/shard_map/all_to_all | solution.py:26
  26.8 44.7 %all-to-all-start.1 = ((bf16[4,4,2,96,256]{4,3,2,1,0:T(8,128)(2,1)}), bf16[4,4,2,96,256]{4,3,2,1,0:T(8,128)(2,1)}, u32[]{:S(2)}, u32[]{:S(2)}) async-start(bf16[4,4,2,96,256]{4,3,2,1,0:T(8,128)(2,1)} %broadcast_in_dim.7), calls=%async_computation.1 | async-start | bytes 3145728 | tf_op jit(solution)/shard_map/all_to_all | solution.py:26
  31.2 7.8 %collective-permute-start.4 = (bf16[3,96,384]{2,1,0:T(8,128)(2,1)S(1)}, bf16[3,96,384]{2,1,0:T(8,128)(2,1)S(1)}, u32[]{:S(2)}, u32[]{:S(2)}) collective-permute-start(bf16[3,96,384]{2,1,0:T(8,128)(2,1)S(1)} %constant_dynamic-slice_fusion.4), channel_id=1, source_target_pairs={{0,32},{32,0},{1,33},{33,1},{2,34},{34,2},{3,35},{35,3},{4,36},{36... | collective-permute-start | bytes 663560 | tf_op jit(solution)/shard_map/ppermute | solution.py:21
  39.1 23.6 %collective-permute-start.6 = (bf16[2,3,96,384]{3,2,1,0:T(8,128)(2,1)S(1)}, bf16[2,3,96,384]{3,2,1,0:T(8,128)(2,1)S(1)}, u32[]{:S(2)}, u32[]{:S(2)}) collective-permute-start(bf16[2,3,96,384]{3,2,1,0:T(8,128)(2,1)S(1)} %get-tuple-element.10), channel_id=1, source_target_pairs={{0,2},{1,3},{2,0},{3,1},{4,6},{5,7},{6,4},{7,5},{8,10},{9,11},{10,... | collective-permute-start | bytes 1327112 | tf_op jit(solution)/shard_map/ppermute | solution.py:21
  44.5 23.3 %collective-permute-start.7 = (bf16[2,3,96,384]{3,2,1,0:T(8,128)(2,1)S(1)}, bf16[2,3,96,384]{3,2,1,0:T(8,128)(2,1)S(1)}, u32[]{:S(2)}, u32[]{:S(2)}) collective-permute-start(bf16[2,3,96,384]{3,2,1,0:T(8,128)(2,1)S(1)} %get-tuple-element.10), channel_id=1, source_target_pairs={{0,3},{1,0},{2,1},{3,2},{4,7},{5,4},{6,5},{7,6},{8,11},{9,8},{10,9... | collective-permute-start | bytes 1327112 | tf_op jit(solution)/shard_map/ppermute | solution.py:21
  47.6 21.6 %collective-permute-start.5 = (bf16[2,3,96,384]{3,2,1,0:T(8,128)(2,1)S(1)}, bf16[2,3,96,384]{3,2,1,0:T(8,128)(2,1)S(1)}, u32[]{:S(2)}, u32[]{:S(2)}) collective-permute-start(bf16[2,3,96,384]{3,2,1,0:T(8,128)(2,1)S(1)} %get-tuple-element.10), channel_id=1, source_target_pairs={{0,1},{1,2},{2,3},{3,0},{4,5},{5,6},{6,7},{7,4},{8,9},{9,10},{10,1... | collective-permute-start | bytes 1327112 | tf_op jit(solution)/shard_map/ppermute | solution.py:21
  69.2 6.9 %copy-start.3 = (bf16[1,48,1536]{2,1,0:T(8,128)(2,1)S(1)}, bf16[1,48,1536]{2,1,0:T(8,128)(2,1)}, u32[]{:S(2)}) copy-start(bf16[1,48,1536]{2,1,0:T(8,128)(2,1)} %param.6) | copy-start | bytes 442372
  69.5 62.6 %copy-start.4 = (s32[8,4]{0,1:T(4,128)S(1)}, s32[8,4]{0,1:T(4,128)}, u32[]{:S(2)}) copy-start(s32[8,4]{0,1:T(4,128)} %param.7) | copy-start | bytes 388
  69.5 70.2 %collective-permute-start.8 = (bf16[4,2,3,96,384]{4,3,2,1,0:T(8,128)(2,1)S(1)}, bf16[4,2,3,96,384]{4,3,2,1,0:T(8,128)(2,1)}, u32[]{:S(2)}, u32[]{:S(2)}) collective-permute-start(bf16[4,2,3,96,384]{4,3,2,1,0:T(8,128)(2,1)S(1)} %pad_maximum_fusion.refs_4_), channel_id=1, source_target_pairs={{0,4},{4,0},{1,5},{5,1},{2,6},{6,2},{3,7},{7,3},{8,12},{12,8},{9,1... | collective-permute-start | bytes 5308424 | tf_op jit(solution)/shard_map/ppermute | solution.py:21
  71.5 73.3 %collective-permute-start.14 = (bf16[4,4,2,96,256]{4,3,2,1,0:T(8,128)(2,1)}, bf16[4,4,2,96,256]{4,3,2,1,0:T(8,128)(2,1)}, u32[]{:S(2)}, u32[]{:S(2)}) collective-permute-start(bf16[4,4,2,96,256]{4,3,2,1,0:T(8,128)(2,1)} %all-to-all-done.1.shared), channel_id=1, source_target_pairs={{0,4},{4,0},{1,5},{5,1},{2,6},{6,2},{3,7},{7,3},{8,12},{12,8},{9,1... | collective-permute-start | bytes 4718600 | tf_op jit(solution)/shard_map/ppermute | solution.py:21
  73.9 16.4 %collective-permute-start.10 = (bf16[2,96,512]{2,1,0:T(8,128)(2,1)S(1)}, bf16[2,96,512]{2,1,0:T(8,128)(2,1)S(1)}, u32[]{:S(2)}, u32[]{:S(2)}) collective-permute-start(bf16[2,96,512]{2,1,0:T(8,128)(2,1)S(1)} %get-tuple-element.12), channel_id=1, source_target_pairs={{0,8},{8,16},{16,24},{24,0},{1,9},{9,17},{17,25},{25,1},{2,10},{10... | collective-permute-start | bytes 589832 | tf_op jit(solution)/shard_map/ppermute | solution.py:21
  76.1 32.2 %collective-permute-start = (bf16[1,48,1536]{2,1,0:T(8,128)(2,1)S(1)}, bf16[1,48,1536]{2,1,0:T(8,128)(2,1)S(1)}, u32[]{:S(2)}, u32[]{:S(2)}) collective-permute-start(bf16[1,48,1536]{2,1,0:T(8,128)(2,1)S(1)} %copy-done.3), channel_id=1, source_target_pairs={{0,256},{256,0},{1,257},{257,1},{2,258},{258,2},{3,259},{259,3},{4... | collective-permute-start | bytes 442376 | tf_op jit(solution)/shard_map/ppermute | solution.py:21
  84.5 20.9 %collective-permute-start.11 = (bf16[2,96,512]{2,1,0:T(8,128)(2,1)S(1)}, bf16[2,96,512]{2,1,0:T(8,128)(2,1)S(1)}, u32[]{:S(2)}, u32[]{:S(2)}) collective-permute-start(bf16[2,96,512]{2,1,0:T(8,128)(2,1)S(1)} %get-tuple-element.12), channel_id=1, source_target_pairs={{0,16},{8,24},{16,0},{24,8},{1,17},{9,25},{17,1},{25,9},{2,18},{10... | collective-permute-start | bytes 589832 | tf_op jit(solution)/shard_map/ppermute | solution.py:21
  90.3 15.9 %collective-permute-start.12 = (bf16[2,96,512]{2,1,0:T(8,128)(2,1)S(1)}, bf16[2,96,512]{2,1,0:T(8,128)(2,1)S(1)}, u32[]{:S(2)}, u32[]{:S(2)}) collective-permute-start(bf16[2,96,512]{2,1,0:T(8,128)(2,1)S(1)} %get-tuple-element.12), channel_id=1, source_target_pairs={{0,24},{8,0},{16,8},{24,16},{1,25},{9,1},{17,9},{25,17},{2,26},{10... | collective-permute-start | bytes 589832 | tf_op jit(solution)/shard_map/ppermute | solution.py:21
  106.4 38.5 %collective-permute-start.13 = (bf16[4,2,96,512]{3,2,1,0:T(8,128)(2,1)S(1)}, bf16[4,2,96,512]{3,2,1,0:T(8,128)(2,1)}, u32[]{:S(2)}, u32[]{:S(2)}) collective-permute-start(bf16[4,2,96,512]{3,2,1,0:T(8,128)(2,1)S(1)} %pad_maximum_fusion.1.direct), channel_id=1, source_target_pairs={{0,4},{4,0},{1,5},{5,1},{2,6},{6,2},{3,7},{7,3},{8,12},{12,8},{9,1... | collective-permute-start | bytes 2359304 | tf_op jit(solution)/shard_map/ppermute | solution.py:21
  108.3 18.1 %collective-permute-start.1 = (bf16[2,48,1536]{2,1,0:T(8,128)(2,1)S(1)}, bf16[2,48,1536]{2,1,0:T(8,128)(2,1)S(1)}, u32[]{:S(2)}, u32[]{:S(2)}) collective-permute-start(bf16[2,48,1536]{2,1,0:T(8,128)(2,1)S(1)} %constant_dynamic-update-slice_fusion.refs_0_), channel_id=1, source_target_pairs={{0,64},{64,128},{128,192},{192,0},{1,65},{65,129},{129,193},{193,1... | collective-permute-start | bytes 884744 | tf_op jit(solution)/shard_map/ppermute | solution.py:21
  112.8 24.5 %collective-permute-start.2 = (bf16[2,48,1536]{2,1,0:T(8,128)(2,1)S(1)}, bf16[2,48,1536]{2,1,0:T(8,128)(2,1)}, u32[]{:S(2)}, u32[]{:S(2)}) collective-permute-start(bf16[2,48,1536]{2,1,0:T(8,128)(2,1)S(1)} %constant_dynamic-update-slice_fusion.refs_0_), channel_id=1, source_target_pairs={{0,128},{64,192},{128,0},{192,64},{1,129},{65,193},{129,1},{193,65... | collective-permute-start | bytes 884744 | tf_op jit(solution)/shard_map/ppermute | solution.py:21
  126.5 0.7 copy-start.1
  127.2 12.5 %collective-permute-start.3 = (bf16[2,48,1536]{2,1,0:T(8,128)(2,1)S(1)}, bf16[2,48,1536]{2,1,0:T(8,128)(2,1)}, u32[]{:S(2)}, u32[]{:S(2)}) collective-permute-start(bf16[2,48,1536]{2,1,0:T(8,128)(2,1)S(1)} %constant_dynamic-update-slice_fusion.refs_0_), channel_id=1, source_target_pairs={{0,192},{64,0},{128,64},{192,128},{1,193},{65,1},{129,65},{193,129... | collective-permute-start | bytes 884744 | tf_op jit(solution)/shard_map/ppermute | solution.py:21
  139.7 1.0 copy-start.2

commit v3 on v1

v3 whole, which is shorter than its diff:
```python
import jax
import jax.numpy as jnp
from jax import lax
from jax.experimental import pallas as pl
from jax.experimental.pallas import tpu as pltpu
from jax.sharding import Mesh
from jax.sharding import PartitionSpec as P

AXES = ("zh", "y", "zl", "core", "x")
VA = ("zh", "y")
F32 = jnp.float32
BF16 = jnp.bfloat16
VMEM = pl.BlockSpec(memory_space=pltpu.VMEM)
SMEM = pl.BlockSpec(memory_space=pltpu.SMEM)
PARAMS = pltpu.CompilerParams(vmem_limit_bytes=20 << 20)


def shifted(block, axis, by):
    n = lax.axis_size(axis)
    return lax.ppermute(block, axis, [(i, (i + by) % n) for i in range(n)])


def copies_from(array, axis):
    copies = jnp.broadcast_to(array, (lax.axis_size(axis), *array.shape))
    return lax.all_to_all(copies, axis, 0, 0, tiled=True)


def half_kernel(lists, where, *refs):
    kets, (mine, theirs, half, ket) = refs[:8], refs[8:]
    zh, y, _, core, x = [where[i] for i in range(5)]
    cols = ket.shape[1]
    parts, own, rows, width = mine.shape
    for d in range(8):
        for h in range(2):
            ket[2 * d + h] = kets[d][h]
    places, groups = [], []
    for r in range(2):
        side = core if r == 0 else 1 - core
        for z in range(4):
            for j in range(2):
                q = 4 * z + 2 * side + j
                high = q // 8
                places.append(2 * ((y - q % 8 + 8) % 8) + jnp.where(high == zh, 0, 1))
                groups.append(2 * z + side)
    n_q = len(places)
    out = None
    for s in range(parts):
        at = pl.multiple_of(((x - s + 4) % 4) * width, 128)
        lhs = jnp.concatenate([ket[q, :, pl.ds(at, width)] for q in places], axis=0)
        rhs = jnp.concatenate([mine[s], theirs[s]], axis=0).reshape(2 * own * rows, width)
        term = lax.dot_general(lhs, rhs, (((1,), (1,)), ((), ())), preferred_element_type=F32)
        out = term if out is None else out + term
    for side in range(2):
        first = own * (core if side == 0 else 1 - core)
        for k in range(own):
            p = first + k
            at = (side * own + k) * rows
            for i in range(n_q):
                wanted = lists[groups[i], 0] == p
                for m in range(1, lists.shape[1]):
                    wanted = jnp.logical_or(wanted, lists[groups[i], m] == p)
                block = out[i * cols : (i + 1) * cols, at : at + rows]
                block = jnp.where(wanted, block, 0.0).astype(BF16)
                half[pl.ds(pl.multiple_of(p * cols, 16), cols), i * rows : (i + 1) * rows] = block


def total_kernel(half, mine, theirs, out):
    parts, places, blocks, rows, width = mine.shape
    m = half.shape[0]
    keep = m * rows // 128
    lhs = half[...]
    for x in range(parts):
        rhs = jnp.concatenate([ref[x].reshape(places * blocks * rows, width) for ref in (mine, theirs)], axis=0)
        sums = jnp.dot(lhs, rhs, preferred_element_type=F32)
        for i in range(width // rows):
            block = sums[:, i * rows : (i + 1) * rows]
            tail = jnp.concatenate([block[keep:, 32 * s : 32 * s + 32] for s in range(rows // 32)], axis=0)
            out[x * (width // rows) + i] = jnp.concatenate([block[:keep], tail], axis=1).astype(BF16)


def sum_kernel(parts, out):
    rows = out.shape[1]
    keep, step = parts.shape[1], out.shape[0] - parts.shape[1]
    sums = parts[0].astype(F32)
    for i in range(1, parts.shape[0]):
        sums = sums + parts[i].astype(F32)
    out[:keep, :] = sums[:, :rows]
    tail = [sums[step * s : step * (s + 1), rows:] for s in range(rows // 32)]
    out[keep:, :] = jnp.concatenate(tail, axis=1)


def per_device(amplitudes, bra_factor, ket_factor, pair_list):
    pairs, rows, _ = amplitudes.shape
    cols = ket_factor.shape[1]
    n_a = bra_factor.shape[2]
    core = lax.axis_index("core")
    where = jnp.stack([lax.axis_index(name) for name in AXES]).astype(jnp.int32)
    n_own = n_a // lax.axis_size("x")

    ket = jnp.concatenate([ket_factor, shifted(ket_factor, "zh", 1)], axis=0)
    ahead, behind = [ket], [ket]
    for s in range(1, 5):
        ahead.append(shifted(ahead[-1], "y", 1))
        if s < 4:
            behind.append(shifted(behind[-1], "y", -1))
    kets = ahead + behind[:0:-1]
    own = lax.dynamic_slice_in_dim(bra_factor, n_own * lax.axis_index("x"), n_own, 2)
    bra = copies_from(copies_from(own, "zl"), "x")
    tau = lax.dynamic_slice_in_dim(amplitudes, core * (pairs // 2), pairs // 2, 0)
    mine = jnp.stack([tau] + [shifted(tau, "x", s) for s in range(1, 4)])
    theirs = shifted(mine, "core", 1)
    bra_other = shifted(bra, "core", 1)

    n_q = 2 * bra.shape[1] * bra.shape[2]
    half = pl.pallas_call(
        half_kernel,
        in_specs=[SMEM, SMEM] + [VMEM] * (len(kets) + 2),
        out_specs=VMEM,
        out_shape=jax.ShapeDtypeStruct((pairs * cols, n_q * rows), BF16),
        scratch_shapes=[pltpu.VMEM((n_q, cols, ket.shape[2]), BF16)],
        compiler_params=PARAMS,
        name="half",
    )(pair_list, where, *kets, mine, theirs)
    n_va = n_a // rows
    total = pl.pallas_call(
        total_kernel,
        in_specs=[VMEM] * 3,
        out_specs=VMEM,
        out_shape=jax.ShapeDtypeStruct((n_va, pairs * cols * rows // 128, 128), BF16),
        compiler_params=PARAMS,
        name="total",
    )(half, bra, bra_other)
    total = lax.all_to_all(total, VA, 0, 0, tiled=True)
    out = pl.pallas_call(
        sum_kernel,
        in_specs=[VMEM],
        out_specs=VMEM,
        out_shape=jax.ShapeDtypeStruct((pairs * cols, rows), F32),
        compiler_params=PARAMS,
        name="sum",
    )(total)
    return out.reshape(pairs, cols, rows).transpose(0, 2, 1)


def solution(mesh):
    torus = Mesh(mesh.devices.reshape(2, 8, 4, 2, 4), AXES)
    return jax.shard_map(
        per_device,
        mesh=torus,
        in_specs=(P(None, VA, "x"), P(("zl", "core"), VA, None), P(VA, ("zl", "core", "x"), None), P()),
        out_specs=P(None, VA, ("zl", "core", "x")),
        check_vma=False,
    )
```

time: 147 us -> 176 us (1.20)
  the two profiles are of different devices: /device:TPU:74 before, /device:TPU:72 now
where the time goes in v3:
time: 176 us; the launch traced here: 175 us
  blocking collectives  93 us (53%)
  starting transfers between devices  42.8 us (24%)
  waiting for transfers between devices  22.7 us (13%)
  Pallas kernels  9.49 us (5%)
  local copies, waits for them, and re-layouts  6.01 us (3%)
    all_to_all x2, blocking collectives, copies_from(): return lax.all_to_all(copies, axis, 0, 0, tiled=True)  53.1 us
    ppermute x13, starting transfers between devices, shifted(): return lax.ppermute(block, axis, [(i, (i + by) % n) for i in range(n)])  42.8 us
    all_to_all x1, blocking collectives, per_device(): total = lax.all_to_all(total, VA, 0, 0, tiled=True)  39.9 us
    ppermute x13, waiting for transfers between devices, shifted(): return lax.ppermute(block, axis, [(i, (i + by) % n) for i in range(n)])  22.7 us
    pallas_call x1, Pallas kernels, per_device(): pl.pallas_call(half_kernel, in_specs=[SMEM, SMEM] + [VMEM] * (len(kets) +...  4.69 us
    unnamed x18, local copies, waits for them, and re-layouts  4.53 us
    pallas_call x1, Pallas kernels, per_device(): pl.pallas_call(total_kernel, in_specs=[VMEM] * 3, out_specs=VMEM, out_sha...  3.95 us
  transfers between devices with their start and end apart: 13, of which 7 were waited for; matrix products, arithmetic and copies ran while one was open for 1% of the time, Pallas kernels for 3%

profile of v3, /device:TPU:72, one launch (start us, length us, event | category | flops | bytes accessed | tf_op | source)
XLA Modules:
  0.0 175.4 jit_solution(489769492577265022)
XLA Ops:
  0.0 1.1 copy-done
  1.1 21.0 %all_to_all.15 = bf16[4,2,96,384]{3,2,1,0:T(8,128)(2,1)S(1)} all-to-all(bf16[4,2,96,384]{3,2,1,0:T(8,128)(2,1)S(1)} %broadcast_in_dim.6), channel_id=1, replica_groups=mesh['zh'=2,'y'=8,'zl'=4,'core'=2,'x'=4] {'zl'}, dimensions={0} | all-to-all | bytes 1179648 | tf_op jit(solution)/shard_map/all_to_all | solution.py:25
  22.5 32.1 %all_to_all.16.mine = bf16[4,4,2,96,384]{4,3,2,1,0:T(8,128)(2,1)S(1)} all-to-all(bf16[4,4,2,96,384]{4,3,2,1,0:T(8,128)(2,1)S(1)} %broadcast_in_dim.7), channel_id=1, replica_groups=mesh['zh'=2,'y'=8,'zl'=4,'core'=2,'x'=4] {'x'}, dimensions={0} | all-to-all | bytes 4718592 | tf_op jit(solution)/shard_map/all_to_all | solution.py:25
  54.6 2.0 %collective-permute-start.12 = (bf16[4,4,2,96,384]{4,3,2,1,0:T(8,128)(2,1)S(1)}, bf16[4,4,2,96,384]{4,3,2,1,0:T(8,128)(2,1)}, u32[]{:S(2)}, u32[]{:S(2)}) collective-permute-start(bf16[4,4,2,96,384]{4,3,2,1,0:T(8,128)(2,1)S(1)} %all_to_all.16.mine), channel_id=1, source_target_pairs={{0,4},{4,0},{1,5},{5,1},{2,6},{6,2},{3,7},{7,3},{8,12},{12,8},{9,1... | collective-permute-start | bytes 7077896 | tf_op jit(solution)/shard_map/ppermute | solution.py:20
  56.7 2.7 %collective-permute-start.9 = (bf16[3,96,384]{2,1,0:T(8,128)(2,1)S(1)}, bf16[3,96,384]{2,1,0:T(8,128)(2,1)S(1)}, u32[]{:S(2)}, u32[]{:S(2)}) collective-permute-start(bf16[3,96,384]{2,1,0:T(8,128)(2,1)S(1)} %constant_dynamic-slice_fusion.1), channel_id=1, source_target_pairs={{0,2},{1,3},{2,0},{3,1},{4,6},{5,7},{6,4},{7,5},{8,10},{9,11},{10,... | collective-permute-start | bytes 663560 | tf_op jit(solution)/shard_map/ppermute | solution.py:20
  59.4 3.1 %collective-permute-start.8 = (bf16[3,96,384]{2,1,0:T(8,128)(2,1)S(1)}, bf16[3,96,384]{2,1,0:T(8,128)(2,1)S(1)}, u32[]{:S(2)}, u32[]{:S(2)}) collective-permute-start(bf16[3,96,384]{2,1,0:T(8,128)(2,1)S(1)} %constant_dynamic-slice_fusion.1), channel_id=1, source_target_pairs={{0,1},{1,2},{2,3},{3,0},{4,5},{5,6},{6,7},{7,4},{8,9},{9,10},{10,1... | collective-permute-start | bytes 663560 | tf_op jit(solution)/shard_map/ppermute | solution.py:20
  62.5 3.9 %collective-permute-start.10 = (bf16[3,96,384]{2,1,0:T(8,128)(2,1)S(1)}, bf16[3,96,384]{2,1,0:T(8,128)(2,1)S(1)}, u32[]{:S(2)}, u32[]{:S(2)}) collective-permute-start(bf16[3,96,384]{2,1,0:T(8,128)(2,1)S(1)} %constant_dynamic-slice_fusion.1), channel_id=1, source_target_pairs={{0,3},{1,0},{2,1},{3,2},{4,7},{5,4},{6,5},{7,6},{8,11},{9,8},{10,9... | collective-permute-start | bytes 663560 | tf_op jit(solution)/shard_map/ppermute | solution.py:20
  66.5 8.2 %collective-permute-start = (bf16[1,48,1536]{2,1,0:T(8,128)(2,1)S(1)}, bf16[1,48,1536]{2,1,0:T(8,128)(2,1)S(1)}, u32[]{:S(2)}, u32[]{:S(2)}) collective-permute-start(bf16[1,48,1536]{2,1,0:T(8,128)(2,1)S(1)} %copy-done.6), channel_id=1, source_target_pairs={{0,256},{256,0},{1,257},{257,1},{2,258},{258,2},{3,259},{259,3},{4... | collective-permute-start | bytes 442376 | tf_op jit(solution)/shard_map/ppermute | solution.py:20
  74.7 6.9 %collective-permute-done = bf16[1,48,1536]{2,1,0:T(8,128)(2,1)S(1)} collective-permute-done((bf16[1,48,1536]{2,1,0:T(8,128)(2,1)S(1)}, bf16[1,48,1536]{2,1,0:T(8,128)(2,1)S(1)}, u32[]{:S(2)}, u32[]{:S(2)}) %collective-permute-start) | collective-permute-done | bytes 147488 | tf_op jit(solution)/shard_map/ppermute | solution.py:20
  81.7 3.5 %collective-permute-start.1 = (bf16[2,48,1536]{2,1,0:T(8,128)(2,1)S(1)}, bf16[2,48,1536]{2,1,0:T(8,128)(2,1)S(1)}, u32[]{:S(2)}, u32[]{:S(2)}) collective-permute-start(bf16[2,48,1536]{2,1,0:T(8,128)(2,1)S(1)} %constant_dynamic-update-slice_fusion.refs_0_), channel_id=1, source_target_pairs={{0,32},{32,64},{64,96},{96,128},{128,160},{160,192},{192,224},{224... | collective-permute-start | bytes 884744 | tf_op jit(solution)/shard_map/ppermute | solution.py:20
  85.2 1.0 fusion
  86.2 2.4 %collective-permute-start.5 = (bf16[2,48,1536]{2,1,0:T(8,128)(2,1)S(1)}, bf16[2,48,1536]{2,1,0:T(8,128)(2,1)S(1)}, u32[]{:S(2)}, u32[]{:S(2)}) collective-permute-start(bf16[2,48,1536]{2,1,0:T(8,128)(2,1)S(1)} %constant_dynamic-update-slice_fusion.refs_0_), channel_id=1, source_target_pairs={{0,224},{32,0},{64,32},{96,64},{128,96},{160,128},{192,160},{224,1... | collective-permute-start | bytes 884744 | tf_op jit(solution)/shard_map/ppermute | solution.py:20
  88.6 1.1 pad_maximum_fusion.refs_8_
  89.6 1.8 %collective-permute-done.1.refs_1_ = bf16[2,48,1536]{2,1,0:T(8,128)(2,1)S(1)} collective-permute-done((bf16[2,48,1536]{2,1,0:T(8,128)(2,1)S(1)}, bf16[2,48,1536]{2,1,0:T(8,128)(2,1)S(1)}, u32[]{:S(2)}, u32[]{:S(2)}) %collective-permute-start.1) | collective-permute-done | bytes 294944 | tf_op jit(solution)/shard_map/ppermute | solution.py:20
  91.4 3.5 %collective-permute-start.2 = (bf16[2,48,1536]{2,1,0:T(8,128)(2,1)S(1)}, bf16[2,48,1536]{2,1,0:T(8,128)(2,1)S(1)}, u32[]{:S(2)}, u32[]{:S(2)}) collective-permute-start(bf16[2,48,1536]{2,1,0:T(8,128)(2,1)S(1)} %collective-permute-done.1.refs_1_), channel_id=1, source_target_pairs={{0,32},{32,64},{64,96},{96,128},{128,160},{160,192},{192,224},{224... | collective-permute-start | bytes 884744 | tf_op jit(solution)/shard_map/ppermute | solution.py:20
  94.9 1.9 %collective-permute-start.11 = (bf16[4,3,96,384]{3,2,1,0:T(8,128)(2,1)}, bf16[4,3,96,384]{3,2,1,0:T(8,128)(2,1)}, u32[]{:S(2)}, u32[]{:S(2)}) collective-permute-start(bf16[4,3,96,384]{3,2,1,0:T(8,128)(2,1)} %pad_maximum_fusion.refs_8_), channel_id=1, source_target_pairs={{0,4},{4,0},{1,5},{5,1},{2,6},{6,2},{3,7},{7,3},{8,12},{12,8},{9,1... | collective-permute-start | bytes 2654216 | tf_op jit(solution)/shard_map/ppermute | solution.py:20
  96.9 2.5 %collective-permute-start.6 = (bf16[2,48,1536]{2,1,0:T(8,128)(2,1)S(1)}, bf16[2,48,1536]{2,1,0:T(8,128)(2,1)}, u32[]{:S(2)}, u32[]{:S(2)}) collective-permute-start(bf16[2,48,1536]{2,1,0:T(8,128)(2,1)S(1)} %collective-permute-done.5.refs_7_), channel_id=1, source_target_pairs={{0,224},{32,0},{64,32},{96,64},{128,96},{160,128},{192,160},{224,1... | collective-permute-start | bytes 884744 | tf_op jit(solution)/shard_map/ppermute | solution.py:20
  99.4 0.7 copy-done.1
  100.1 0.9 collective-permute-done.2.refs_2_
  101.0 2.7 %collective-permute-start.3 = (bf16[2,48,1536]{2,1,0:T(8,128)(2,1)S(1)}, bf16[2,48,1536]{2,1,0:T(8,128)(2,1)}, u32[]{:S(2)}, u32[]{:S(2)}) collective-permute-start(bf16[2,48,1536]{2,1,0:T(8,128)(2,1)S(1)} %collective-permute-done.2.refs_2_), channel_id=1, source_target_pairs={{0,32},{32,64},{64,96},{96,128},{128,160},{160,192},{192,224},{224... | collective-permute-start | bytes 884744 | tf_op jit(solution)/shard_map/ppermute | solution.py:20
  104.5 3.9 %collective-permute-done.6.refs_6_ = bf16[2,48,1536]{2,1,0:T(8,128)(2,1)} collective-permute-done((bf16[2,48,1536]{2,1,0:T(8,128)(2,1)S(1)}, bf16[2,48,1536]{2,1,0:T(8,128)(2,1)}, u32[]{:S(2)}, u32[]{:S(2)}) %collective-permute-start.6) | collective-permute-done | bytes 294944 | tf_op jit(solution)/shard_map/ppermute | solution.py:20
  108.4 3.0 %collective-permute-start.7 = (bf16[2,48,1536]{2,1,0:T(8,128)(2,1)}, bf16[2,48,1536]{2,1,0:T(8,128)(2,1)}, u32[]{:S(2)}, u32[]{:S(2)}) collective-permute-start(bf16[2,48,1536]{2,1,0:T(8,128)(2,1)} %collective-permute-done.6.refs_6_), channel_id=1, source_target_pairs={{0,224},{32,0},{64,32},{96,64},{128,96},{160,128},{192,160},{224,1... | collective-permute-start | bytes 884744 | tf_op jit(solution)/shard_map/ppermute | solution.py:20
  111.4 1.3 collective-permute-done.3.refs_3_
  112.7 3.2 %collective-permute-start.4 = (bf16[2,48,1536]{2,1,0:T(8,128)(2,1)}, bf16[2,48,1536]{2,1,0:T(8,128)(2,1)}, u32[]{:S(2)}, u32[]{:S(2)}) collective-permute-start(bf16[2,48,1536]{2,1,0:T(8,128)(2,1)} %collective-permute-done.3.refs_3_), channel_id=1, source_target_pairs={{0,32},{32,64},{64,96},{96,128},{128,160},{160,192},{192,224},{224... | collective-permute-start | bytes 884744 | tf_op jit(solution)/shard_map/ppermute | solution.py:20
  116.1 5.3 %collective-permute-done.7.refs_5_ = bf16[2,48,1536]{2,1,0:T(8,128)(2,1)} collective-permute-done((bf16[2,48,1536]{2,1,0:T(8,128)(2,1)}, bf16[2,48,1536]{2,1,0:T(8,128)(2,1)}, u32[]{:S(2)}, u32[]{:S(2)}) %collective-permute-start.7) | collective-permute-done | bytes 294944 | tf_op jit(solution)/shard_map/ppermute | solution.py:20
  121.4 2.6 %collective-permute-done.4.refs_4_ = bf16[2,48,1536]{2,1,0:T(8,128)(2,1)} collective-permute-done((bf16[2,48,1536]{2,1,0:T(8,128)(2,1)}, bf16[2,48,1536]{2,1,0:T(8,128)(2,1)}, u32[]{:S(2)}, u32[]{:S(2)}) %collective-permute-start.4) | collective-permute-done | bytes 294944 | tf_op jit(solution)/shard_map/ppermute | solution.py:20
  124.0 1.0 copy-done.2
  125.0 1.0 copy-done.4
  125.9 4.7 %half.1 = bf16[288,1536]{1,0:T(8,128)(2,1)S(1)} custom-call(s32[8,4]{1,0:T(8,128)S(1)} %copy.5.lists, s32[5]{0:T(128)S(1)} %stack.38.where, bf16[2,48,1536]{2,1,0:T(8,128)(2,1)S(1)} %constant_dynamic-update-slice_fusion.refs_0_, bf16[2,48,1536]{2,1,0:T(8,128)(2,1)S(1)} %collective-permute-done.1.refs_1_, bf16[2,48,1536]{2,1,0:T(8,128)(2,1)S(1)} %copy-done.4, ...), custom_call_target="tpu_custom_call" | custom-call | tf_op jit(solution)/shard_map/half/pallas_call | solution.py:115
  130.6 4.0 %total.1 = bf16[16,216,128]{2,1,0:T(8,128)(2,1)S(1)} custom-call(bf16[288,1536]{1,0:T(8,128)(2,1)S(1)} %half.1, bf16[4,4,2,96,384]{4,3,2,1,0:T(8,128)(2,1)S(1)} %all_to_all.16.mine, bf16[4,4,2,96,384]{4,3,2,1,0:T(8,128)(2,1)} %collective-permute-done.12.theirs), custom_call_target="tpu_custom_call" | custom-call | tf_op jit(solution)/shard_map/total/pallas_call | solution.py:125
  134.6 39.9 %all_to_all.17.parts = bf16[16,216,128]{2,1,0:T(8,128)(2,1)S(1)} all-to-all(bf16[16,216,128]{2,1,0:T(8,128)(2,1)S(1)} %total.1), channel_id=1, replica_groups=mesh['zh'=2,'y'=8,'zl'=4,'core'=2,'x'=4] {'zh','y'}, dimensions={0} | all-to-all | bytes 1769472 | tf_op jit(solution)/shard_map/all_to_all | solution.py:133
  174.5 0.8 sum.1
  (26 shorter events, 1.4 us)
Async XLA Ops:
  0.0 1.1 copy-start
  22.4 34.2 %copy-start.5 = (bf16[6,96,384]{2,1,0:T(8,128)(2,1)S(1)}, bf16[6,96,384]{2,1,0:T(8,128)(2,1)}, u32[]{:S(2)}) copy-start(bf16[6,96,384]{2,1,0:T(8,128)(2,1)} %param.4) | copy-start | bytes 1327108
  22.5 44.0 %copy-start.6 = (bf16[1,48,1536]{2,1,0:T(8,128)(2,1)S(1)}, bf16[1,48,1536]{2,1,0:T(8,128)(2,1)}, u32[]{:S(2)}) copy-start(bf16[1,48,1536]{2,1,0:T(8,128)(2,1)} %param.6) | copy-start | bytes 442372
  54.6 61.4 %copy-start.7 = (s32[8,4]{0,1:T(4,128)S(1)}, s32[8,4]{0,1:T(4,128)}, u32[]{:S(2)}) copy-start(s32[8,4]{0,1:T(4,128)} %param.7) | copy-start | bytes 388
  54.6 76.0 %collective-permute-start.12 = (bf16[4,4,2,96,384]{4,3,2,1,0:T(8,128)(2,1)S(1)}, bf16[4,4,2,96,384]{4,3,2,1,0:T(8,128)(2,1)}, u32[]{:S(2)}, u32[]{:S(2)}) collective-permute-start(bf16[4,4,2,96,384]{4,3,2,1,0:T(8,128)(2,1)S(1)} %all_to_all.16.mine), channel_id=1, source_target_pairs={{0,4},{4,0},{1,5},{5,1},{2,6},{6,2},{3,7},{7,3},{8,12},{12,8},{9,1... | collective-permute-start | bytes 7077896 | tf_op jit(solution)/shard_map/ppermute | solution.py:20
  56.7 29.5 %collective-permute-start.9 = (bf16[3,96,384]{2,1,0:T(8,128)(2,1)S(1)}, bf16[3,96,384]{2,1,0:T(8,128)(2,1)S(1)}, u32[]{:S(2)}, u32[]{:S(2)}) collective-permute-start(bf16[3,96,384]{2,1,0:T(8,128)(2,1)S(1)} %constant_dynamic-slice_fusion.1), channel_id=1, source_target_pairs={{0,2},{1,3},{2,0},{3,1},{4,6},{5,7},{6,4},{7,5},{8,10},{9,11},{10,... | collective-permute-start | bytes 663560 | tf_op jit(solution)/shard_map/ppermute | solution.py:20
  59.4 29.1 %collective-permute-start.8 = (bf16[3,96,384]{2,1,0:T(8,128)(2,1)S(1)}, bf16[3,96,384]{2,1,0:T(8,128)(2,1)S(1)}, u32[]{:S(2)}, u32[]{:S(2)}) collective-permute-start(bf16[3,96,384]{2,1,0:T(8,128)(2,1)S(1)} %constant_dynamic-slice_fusion.1), channel_id=1, source_target_pairs={{0,1},{1,2},{2,3},{3,0},{4,5},{5,6},{6,7},{7,4},{8,9},{9,10},{10,1... | collective-permute-start | bytes 663560 | tf_op jit(solution)/shard_map/ppermute | solution.py:20
  62.5 26.0 %collective-permute-start.10 = (bf16[3,96,384]{2,1,0:T(8,128)(2,1)S(1)}, bf16[3,96,384]{2,1,0:T(8,128)(2,1)S(1)}, u32[]{:S(2)}, u32[]{:S(2)}) collective-permute-start(bf16[3,96,384]{2,1,0:T(8,128)(2,1)S(1)} %constant_dynamic-slice_fusion.1), channel_id=1, source_target_pairs={{0,3},{1,0},{2,1},{3,2},{4,7},{5,4},{6,5},{7,6},{8,11},{9,8},{10,9... | collective-permute-start | bytes 663560 | tf_op jit(solution)/shard_map/ppermute | solution.py:20
  66.5 15.2 %collective-permute-start = (bf16[1,48,1536]{2,1,0:T(8,128)(2,1)S(1)}, bf16[1,48,1536]{2,1,0:T(8,128)(2,1)S(1)}, u32[]{:S(2)}, u32[]{:S(2)}) collective-permute-start(bf16[1,48,1536]{2,1,0:T(8,128)(2,1)S(1)} %copy-done.6), channel_id=1, source_target_pairs={{0,256},{256,0},{1,257},{257,1},{2,258},{258,2},{3,259},{259,3},{4... | collective-permute-start | bytes 442376 | tf_op jit(solution)/shard_map/ppermute | solution.py:20
  81.7 9.7 %collective-permute-start.1 = (bf16[2,48,1536]{2,1,0:T(8,128)(2,1)S(1)}, bf16[2,48,1536]{2,1,0:T(8,128)(2,1)S(1)}, u32[]{:S(2)}, u32[]{:S(2)}) collective-permute-start(bf16[2,48,1536]{2,1,0:T(8,128)(2,1)S(1)} %constant_dynamic-update-slice_fusion.refs_0_), channel_id=1, source_target_pairs={{0,32},{32,64},{64,96},{96,128},{128,160},{160,192},{192,224},{224... | collective-permute-start | bytes 884744 | tf_op jit(solution)/shard_map/ppermute | solution.py:20
  86.2 10.7 %collective-permute-start.5 = (bf16[2,48,1536]{2,1,0:T(8,128)(2,1)S(1)}, bf16[2,48,1536]{2,1,0:T(8,128)(2,1)S(1)}, u32[]{:S(2)}, u32[]{:S(2)}) collective-permute-start(bf16[2,48,1536]{2,1,0:T(8,128)(2,1)S(1)} %constant_dynamic-update-slice_fusion.refs_0_), channel_id=1, source_target_pairs={{0,224},{32,0},{64,32},{96,64},{128,96},{160,128},{192,160},{224,1... | collective-permute-start | bytes 884744 | tf_op jit(solution)/shard_map/ppermute | solution.py:20
  91.4 9.6 %collective-permute-start.2 = (bf16[2,48,1536]{2,1,0:T(8,128)(2,1)S(1)}, bf16[2,48,1536]{2,1,0:T(8,128)(2,1)S(1)}, u32[]{:S(2)}, u32[]{:S(2)}) collective-permute-start(bf16[2,48,1536]{2,1,0:T(8,128)(2,1)S(1)} %collective-permute-done.1.refs_1_), channel_id=1, source_target_pairs={{0,32},{32,64},{64,96},{96,128},{128,160},{160,192},{192,224},{224... | collective-permute-start | bytes 884744 | tf_op jit(solution)/shard_map/ppermute | solution.py:20
  94.9 26.5 %collective-permute-start.11 = (bf16[4,3,96,384]{3,2,1,0:T(8,128)(2,1)}, bf16[4,3,96,384]{3,2,1,0:T(8,128)(2,1)}, u32[]{:S(2)}, u32[]{:S(2)}) collective-permute-start(bf16[4,3,96,384]{3,2,1,0:T(8,128)(2,1)} %pad_maximum_fusion.refs_8_), channel_id=1, source_target_pairs={{0,4},{4,0},{1,5},{5,1},{2,6},{6,2},{3,7},{7,3},{8,12},{12,8},{9,1... | collective-permute-start | bytes 2654216 | tf_op jit(solution)/shard_map/ppermute | solution.py:20
  96.9 11.6 %collective-permute-start.6 = (bf16[2,48,1536]{2,1,0:T(8,128)(2,1)S(1)}, bf16[2,48,1536]{2,1,0:T(8,128)(2,1)}, u32[]{:S(2)}, u32[]{:S(2)}) collective-permute-start(bf16[2,48,1536]{2,1,0:T(8,128)(2,1)S(1)} %collective-permute-done.5.refs_7_), channel_id=1, source_target_pairs={{0,224},{32,0},{64,32},{96,64},{128,96},{160,128},{192,160},{224,1... | collective-permute-start | bytes 884744 | tf_op jit(solution)/shard_map/ppermute | solution.py:20
  99.4 0.7 copy-start.1
  101.0 11.7 %collective-permute-start.3 = (bf16[2,48,1536]{2,1,0:T(8,128)(2,1)S(1)}, bf16[2,48,1536]{2,1,0:T(8,128)(2,1)}, u32[]{:S(2)}, u32[]{:S(2)}) collective-permute-start(bf16[2,48,1536]{2,1,0:T(8,128)(2,1)S(1)} %collective-permute-done.2.refs_2_), channel_id=1, source_target_pairs={{0,32},{32,64},{64,96},{96,128},{128,160},{160,192},{192,224},{224... | collective-permute-start | bytes 884744 | tf_op jit(solution)/shard_map/ppermute | solution.py:20
  103.8 0.7 copy-start.3
  108.4 13.0 %collective-permute-start.7 = (bf16[2,48,1536]{2,1,0:T(8,128)(2,1)}, bf16[2,48,1536]{2,1,0:T(8,128)(2,1)}, u32[]{:S(2)}, u32[]{:S(2)}) collective-permute-start(bf16[2,48,1536]{2,1,0:T(8,128)(2,1)} %collective-permute-done.6.refs_6_), channel_id=1, source_target_pairs={{0,224},{32,0},{64,32},{96,64},{128,96},{160,128},{192,160},{224,1... | collective-permute-start | bytes 884744 | tf_op jit(solution)/shard_map/ppermute | solution.py:20
  112.7 11.3 %collective-permute-start.4 = (bf16[2,48,1536]{2,1,0:T(8,128)(2,1)}, bf16[2,48,1536]{2,1,0:T(8,128)(2,1)}, u32[]{:S(2)}, u32[]{:S(2)}) collective-permute-start(bf16[2,48,1536]{2,1,0:T(8,128)(2,1)} %collective-permute-done.3.refs_3_), channel_id=1, source_target_pairs={{0,32},{32,64},{64,96},{96,128},{128,160},{160,192},{192,224},{224... | collective-permute-start | bytes 884744 | tf_op jit(solution)/shard_map/ppermute | solution.py:20
  124.0 1.0 copy-start.2
  125.0 1.0 copy-start.4
